TPU v7x, 32 devices: a whole 2x2x4 slice. The times are simulated.
32 devices in a mesh: wide: 16 (over z, y, x), narrow: 2 (over core).
Axes of the slice: x: 2, y: 2, z: 4, core: 2. Of those that a mesh axis runs over, the one named last changes fastest.
Arguments:
- inputs: float32 [16, 64, 16, 128], P(None, 'wide', 'narrow'), may hold values from -100 to 100
- old_basis: float32 [256, 64, 16, 128], P(None, 'wide', 'narrow'), may hold values from -12 to 12
- conductance: float32 [64, 16, 128], P('wide', 'narrow'), may hold values from 0.5 to 2
- shifts: float32 [3], replicated, may hold values from 0.2 to 4
Outputs:
- new_columns: float32 [48, 64, 16, 128], P(None, 'wide', 'narrow')
- coefficients: float32 [256, 48], replicated
- col_scale: float32 [48], replicated
All inputs are finite; a program needn't handle non-finite values.
Results may differ from a plain program's by a relative error of at most 0.00011.
Values sent between devices are 32-bit elements; how exact they have to be, the bound alone decides.
No kernel may reach another device: no remote copies, remote signals or barrier semaphores. Data moves between devices by JAX's collectives and lax.ppermute only.
A program may use at most 64 MiB of HBM per device.

v0:
```python
import jax
import jax.numpy as jnp
from jax import lax
from jax.sharding import PartitionSpec as P

ITERS = 4


def padded_2(cells, sides, width):
    for axis, dim in sides:
        count = lax.axis_size(axis)
        ends = count - 1
        head = lax.slice_in_dim(cells, 0, width, axis=dim)
        tail = lax.slice_in_dim(cells, cells.shape[dim] - width, cells.shape[dim], axis=dim)
        cells = jnp.concatenate(
            [
                lax.ppermute(tail, axis, [(i, (i + 1) % count) for i in range(ends)]),
                cells,
                lax.ppermute(head, axis, [((i + 1) % count, i) for i in range(ends)]),
            ],
            axis=dim,
        )
    return cells


def spread(coef):
    return coef[:, None, None, None]


def stencil(padded, conductance, shift_col):
    center = padded[:, 1:-1, 1:-1, :]
    deeper = jnp.pad(padded, ((0, 0), (0, 0), (0, 0), (1, 1)))
    beside_all = deeper[:, 2:, 1:-1, 1:-1] + deeper[:, :-2, 1:-1, 1:-1]
    beside_all = beside_all + deeper[:, 1:-1, 2:, 1:-1] + deeper[:, 1:-1, :-2, 1:-1]
    beside_all = beside_all + deeper[:, 1:-1, 1:-1, 2:] + deeper[:, 1:-1, 1:-1, :-2]
    return conductance[None] * (6.0 * center - beside_all) + spread(shift_col) * center


def operate(values, conductance, shift_col):
    padded = padded_2(values, (("wide", 1), ("narrow", 2)), 1)
    return stencil(padded, conductance, shift_col)


def local_dot(left, right):
    return jnp.sum(left * right, axis=(1, 2, 3))


def shards(inputs, old_basis, conductance, shifts):
    total_cells = (
        inputs.shape[1]
        * inputs.shape[2]
        * inputs.shape[3]
        * lax.axis_size("wide")
        * lax.axis_size("narrow")
    )
    shift_col = jnp.repeat(shifts, inputs.shape[0])
    shadow = jnp.tile(inputs, (shifts.shape[0], 1, 1, 1))
    columns = shadow.shape[0]
    solution = jnp.zeros_like(shadow)
    residual = shadow
    search = shadow
    rho_now = lax.psum(local_dot(shadow, shadow), ("wide", "narrow")) / total_cells
    for iteration in range(ITERS):
        search_image = operate(search, conductance, shift_col)
        denominator = lax.psum(local_dot(shadow, search_image), ("wide", "narrow")) / total_cells
        step_alpha = rho_now / denominator
        halfway = residual - spread(step_alpha) * search_image
        halfway_image = operate(halfway, conductance, shift_col)
        cross_sum, square_sum, shadow_half, shadow_image = lax.psum(
            (
                local_dot(halfway_image, halfway),
                local_dot(halfway_image, halfway_image),
                local_dot(shadow, halfway),
                local_dot(shadow, halfway_image),
            ),
            ("wide", "narrow"),
        )
        step_omega = cross_sum / total_cells / (square_sum / total_cells + 1e-06)
        solution = solution + spread(step_alpha) * search + spread(step_omega) * halfway
        residual = halfway - spread(step_omega) * halfway_image
        rho_next = shadow_half / total_cells - step_omega * (shadow_image / total_cells)
        if iteration + 1 < ITERS:
            step_beta = rho_next / rho_now * (step_alpha / step_omega)
            search = residual + spread(step_beta) * (search - spread(step_omega) * search_image)
            rho_now = rho_next
    vflat = old_basis.reshape(old_basis.shape[0], -1)
    wflat = solution.reshape(columns, -1)
    high = lax.Precision.HIGHEST
    first_coef = (
        lax.psum(jnp.einsum("bc,kc->bk", vflat, wflat, precision=high), ("wide", "narrow"))
        / total_cells
    )
    once = wflat - jnp.einsum("bk,bc->kc", first_coef, vflat, precision=high)
    second_coef = (
        lax.psum(jnp.einsum("bc,kc->bk", vflat, once, precision=high), ("wide", "narrow"))
        / total_cells
    )
    twice = once - jnp.einsum("bk,bc->kc", second_coef, vflat, precision=high)
    mean_square = lax.psum(jnp.sum(twice * twice, axis=1), ("wide", "narrow")) / total_cells
    col_scale = jnp.sqrt(mean_square + 1e-06)
    new_columns = (twice / col_scale[:, None]).reshape(solution.shape)
    return (new_columns, first_coef + second_coef, col_scale)


def solution(mesh):
    in_specs = (
        P(None, "wide", "narrow", None),
        P(None, "wide", "narrow", None),
        P("wide", "narrow", None),
        P(),
    )
    out_specs = (P(None, "wide", "narrow", None), P(), P())
    return jax.shard_map(shards, mesh=mesh, in_specs=in_specs, out_specs=out_specs, check_vma=False)
```

profile of v0, /device:TPU:0, one launch (start us, length us, event | category | flops | bytes accessed | tf_op | source)
XLA Modules:
  0.0 634.8 jit_solution(9891462262970364943)
XLA Ops:
  1.9 4.9 collective-permute-start.1
  8.1 2.8 collective-permute-done.1
  10.9 6.2 collective-permute-done
  23.1 40.2 %all-reduce.12 = (f32[48]{0:T(128)S(1)}, f32[48]{0:T(128)S(1)}) all-reduce(f32[48]{0:T(128)S(1)} %get-tuple-element.50, f32[48]{0:T(128)S(1)} %reduce_sum.183), channel_id=1, replica_groups=mesh['wide'=16,'narrow'=2] {'wide','narrow'}, use_global_device_ids=true, to_apply=%region_3.4 | all-reduce | flops 96 | bytes 768 | tf_op jit(solution)/shard_map/psum | solution.py:65
  63.5 4.2 collective-permute-start.5
  69.0 6.1 collective-permute-done.5
  83.2 39.4 %all-reduce.11 = (f32[48]{0:T(128)S(1)}, f32[48]{0:T(128)S(1)}, f32[48]{0:T(128)S(1)}, f32[48]{0:T(128)S(1)}) all-reduce(f32[48]{0:T(128)S(1)} %get-tuple-element.4, f32[48]{0:T(128)S(1)} %get-tuple-element.6, f32[48]{0:T(128)S(1)} %get-tuple-element.5, ...), channel_id=1, replica_groups=mesh['wide'=16,'narrow'=2] {'wide','narrow'}, use_global_device_ids=true, to_apply=%region_5.6 | all-reduce | flops 192 | bytes 1536 | tf_op jit(solution)/shard_map/psum | solution.py:69
  122.9 4.2 collective-permute-start.9
  128.4 6.1 collective-permute-done.9
  142.4 38.4 %psum.160 = f32[48]{0:T(128)S(1)} all-reduce(f32[48]{0:T(128)S(1)} %get-tuple-element.44), channel_id=1, replica_groups=mesh['wide'=16,'narrow'=2] {'wide','narrow'}, use_global_device_ids=true, to_apply=%region_13.14 | all-reduce | flops 48 | bytes 384 | tf_op jit(solution)/shard_map/psum | solution.py:65
  182.2 4.2 collective-permute-start.13
  189.5 5.9 collective-permute-done.12
  202.5 39.3 %all-reduce.10 = (f32[48]{0:T(128)S(1)}, f32[48]{0:T(128)S(1)}, f32[48]{0:T(128)S(1)}, f32[48]{0:T(128)S(1)}) all-reduce(f32[48]{0:T(128)S(1)} %get-tuple-element.14, f32[48]{0:T(128)S(1)} %get-tuple-element.16, f32[48]{0:T(128)S(1)} %get-tuple-element.15, ...), channel_id=1, replica_groups=mesh['wide'=16,'narrow'=2] {'wide','narrow'}, use_global_device_ids=true, to_apply=%region_15.16 | all-reduce | flops 192 | bytes 1536 | tf_op jit(solution)/shard_map/psum | solution.py:69
  243.3 4.2 collective-permute-start.17
  248.8 6.1 collective-permute-done.17
  263.6 38.4 %psum.165 = f32[48]{0:T(128)S(1)} all-reduce(f32[48]{0:T(128)S(1)} %get-tuple-element.38), channel_id=1, replica_groups=mesh['wide'=16,'narrow'=2] {'wide','narrow'}, use_global_device_ids=true, to_apply=%region_23.24 | all-reduce | flops 48 | bytes 384 | tf_op jit(solution)/shard_map/psum | solution.py:65
  303.6 4.2 collective-permute-start.21
  310.9 5.9 collective-permute-done.20
  323.9 39.3 %all-reduce.9 = (f32[48]{0:T(128)S(1)}, f32[48]{0:T(128)S(1)}, f32[48]{0:T(128)S(1)}, f32[48]{0:T(128)S(1)}) all-reduce(f32[48]{0:T(128)S(1)} %get-tuple-element.10, f32[48]{0:T(128)S(1)} %get-tuple-element.12, f32[48]{0:T(128)S(1)} %get-tuple-element.11, ...), channel_id=1, replica_groups=mesh['wide'=16,'narrow'=2] {'wide','narrow'}, use_global_device_ids=true, to_apply=%region_25.26 | all-reduce | flops 192 | bytes 1536 | tf_op jit(solution)/shard_map/psum | solution.py:69
  364.9 4.2 collective-permute-start.25
  370.4 6.1 collective-permute-done.25
  385.2 38.4 %psum.170 = f32[48]{0:T(128)S(1)} all-reduce(f32[48]{0:T(128)S(1)} %get-tuple-element.33), channel_id=1, replica_groups=mesh['wide'=16,'narrow'=2] {'wide','narrow'}, use_global_device_ids=true, to_apply=%region_33.34 | all-reduce | flops 48 | bytes 384 | tf_op jit(solution)/shard_map/psum | solution.py:65
  425.2 4.2 collective-permute-start.29
  432.6 5.9 collective-permute-done.28
  444.5 39.3 %all-reduce.8 = (f32[48]{0:T(128)S(1)}, f32[48]{0:T(128)S(1)}) all-reduce(f32[48]{0:T(128)S(1)} %get-tuple-element.8, f32[48]{0:T(128)S(1)} %get-tuple-element.7), channel_id=1, replica_groups=mesh['wide'=16,'narrow'=2] {'wide','narrow'}, use_global_device_ids=true, to_apply=%region_37.38 | all-reduce | flops 96 | bytes 768 | tf_op jit(solution)/shard_map/psum | solution.py:69
  486.7 5.3 fusion.10
  492.0 40.2 %psum.173 = f32[256,48]{0,1:T(8,128)S(1)} all-reduce(f32[256,48]{0,1:T(8,128)S(1)} %fusion.10), channel_id=1, replica_groups=mesh['wide'=16,'narrow'=2] {'wide','narrow'}, use_global_device_ids=true, to_apply=%region_38.39 | all-reduce | flops 12288 | bytes 98304 | tf_op jit(solution)/shard_map/psum | solution.py:90
  532.2 7.3 %convolution_subtract_fusion.1 = f32[48,4096]{1,0:T(8,128)S(1)} fusion(f32[32,8,32,128]{3,2,1,0:T(8,128)} %bitcast.104, f32[6,8,32,128]{3,2,1,0:T(8,128)S(1)} %bitcast.111, f32[256,48]{0,1:T(8,128)S(1)} %psum.173), kind=kOutput, calls=%fused_computation.16 | convolution fusion | flops 604188672 | bytes 5816320 | tf_op jit(solution)/shard_map/bk,bc->kc/dot_general | solution.py:93
  539.6 5.3 fusion.13
  544.9 41.0 %psum.174 = f32[256,48]{0,1:T(8,128)S(1)} all-reduce(f32[256,48]{0,1:T(8,128)S(1)} %fusion.13), channel_id=1, replica_groups=mesh['wide'=16,'narrow'=2] {'wide','narrow'}, use_global_device_ids=true, to_apply=%region_39.40 | all-reduce | flops 12288 | bytes 98304 | tf_op jit(solution)/shard_map/psum | solution.py:95
  586.6 7.0 %multiply_reduce_fusion = (f32[48]{0:T(128)S(1)}, f32[48,4096]{1,0:T(8,128)S(1)}) fusion(f32[48,4096]{1,0:T(8,128)S(1)} %convolution_subtract_fusion.1, f32[32,8,32,128]{3,2,1,0:T(8,128)} %bitcast.105, f32[256,48]{0,1:T(8,128)S(1)} %psum.174), kind=kOutput, calls=%fused_computation.211 | convolution fusion | flops 604581824 | bytes 5816512 | tf_op jit(solution)/shard_map/bk,bc->kc/dot_general | solution.py:98
  593.6 39.6 %psum.175 = f32[48]{0:T(128)S(1)} all-reduce(f32[48]{0:T(128)S(1)} %get-tuple-element.84), channel_id=1, replica_groups=mesh['wide'=16,'narrow'=2] {'wide','narrow'}, use_global_device_ids=true, to_apply=%region_41.42 | all-reduce | flops 48 | bytes 384 | tf_op jit(solution)/shard_map/psum | solution.py:99
  (127 shorter events, 89.3 us)
Async XLA Ops:
  1.9 9.0 %collective-permute-start.1 = (f32[48,1,8,128]{3,0,2,1:T(8,128)S(1)}, f32[48,1,8,128]{3,0,2,1:T(8,128)S(1)}, u32[]{:S(2)}, u32[]{:S(2)}) collective-permute-start(f32[48,1,8,128]{3,0,2,1:T(8,128)S(1)} %get-tuple-element.82), channel_id=1, source_target_pairs={{0,2},{2,4},{4,6},{6,8},{8,10},{10,12},{12,14},{14,16},{16,18},{18... | collective-permute-start | bytes 589832 | tf_op jit(solution)/shard_map/ppermute | solution.py:17
  6.8 10.3 %collective-permute-start = (f32[48,1,8,128]{3,0,2,1:T(8,128)S(1)}, f32[48,1,8,128]{3,0,2,1:T(8,128)S(1)}, u32[]{:S(2)}, u32[]{:S(2)}) collective-permute-start(f32[48,1,8,128]{3,0,2,1:T(8,128)S(1)} %get-tuple-element.83), channel_id=1, source_target_pairs={{2,0},{4,2},{6,4},{8,6},{10,8},{12,10},{14,12},{16,14},{18,16},{20... | collective-permute-start | bytes 589832 | tf_op jit(solution)/shard_map/ppermute | solution.py:19
  17.1 3.1 collective-permute-start.3
  18.4 3.3 collective-permute-start.2
  63.5 11.6 %collective-permute-start.5 = (f32[48,1,8,128]{3,0,2,1:T(8,128)S(1)}, f32[48,1,8,128]{3,0,2,1:T(8,128)S(1)}, u32[]{:S(2)}, u32[]{:S(2)}) collective-permute-start(f32[48,1,8,128]{3,0,2,1:T(8,128)S(1)} %get-tuple-element.80), channel_id=1, source_target_pairs={{0,2},{2,4},{4,6},{6,8},{8,10},{10,12},{12,14},{14,16},{16,18},{18... | collective-permute-start | bytes 589832 | tf_op jit(solution)/shard_map/ppermute | solution.py:17
  67.7 9.3 %collective-permute-start.4 = (f32[48,1,8,128]{3,0,2,1:T(8,128)S(1)}, f32[48,1,8,128]{3,0,2,1:T(8,128)S(1)}, u32[]{:S(2)}, u32[]{:S(2)}) collective-permute-start(f32[48,1,8,128]{3,0,2,1:T(8,128)S(1)} %get-tuple-element.81), channel_id=1, source_target_pairs={{2,0},{4,2},{6,4},{8,6},{10,8},{12,10},{14,12},{16,14},{18,16},{20... | collective-permute-start | bytes 589832 | tf_op jit(solution)/shard_map/ppermute | solution.py:19
  77.0 2.6 collective-permute-start.7
  78.3 3.3 collective-permute-start.6
  122.9 11.6 %collective-permute-start.9 = (f32[48,1,8,128]{3,0,2,1:T(8,128)S(1)}, f32[48,1,8,128]{3,0,2,1:T(8,128)S(1)}, u32[]{:S(2)}, u32[]{:S(2)}) collective-permute-start(f32[48,1,8,128]{3,0,2,1:T(8,128)S(1)} %get-tuple-element.78), channel_id=1, source_target_pairs={{0,2},{2,4},{4,6},{6,8},{8,10},{10,12},{12,14},{14,16},{16,18},{18... | collective-permute-start | bytes 589832 | tf_op jit(solution)/shard_map/ppermute | solution.py:17
  127.1 9.3 %collective-permute-start.8 = (f32[48,1,8,128]{3,0,2,1:T(8,128)S(1)}, f32[48,1,8,128]{3,0,2,1:T(8,128)S(1)}, u32[]{:S(2)}, u32[]{:S(2)}) collective-permute-start(f32[48,1,8,128]{3,0,2,1:T(8,128)S(1)} %get-tuple-element.79), channel_id=1, source_target_pairs={{2,0},{4,2},{6,4},{8,6},{10,8},{12,10},{14,12},{16,14},{18,16},{20... | collective-permute-start | bytes 589832 | tf_op jit(solution)/shard_map/ppermute | solution.py:19
  136.4 2.6 collective-permute-start.11
  137.7 3.3 collective-permute-start.10
  182.2 7.4 %collective-permute-start.13 = (f32[48,1,8,128]{3,0,2,1:T(8,128)S(1)}, f32[48,1,8,128]{3,0,2,1:T(8,128)S(1)}, u32[]{:S(2)}, u32[]{:S(2)}) collective-permute-start(f32[48,1,8,128]{3,0,2,1:T(8,128)S(1)} %get-tuple-element.76), channel_id=1, source_target_pairs={{0,2},{2,4},{4,6},{6,8},{8,10},{10,12},{12,14},{14,16},{16,18},{18... | collective-permute-start | bytes 589832 | tf_op jit(solution)/shard_map/ppermute | solution.py:17
  186.4 9.1 %collective-permute-start.12 = (f32[48,1,8,128]{3,0,2,1:T(8,128)S(1)}, f32[48,1,8,128]{3,0,2,1:T(8,128)S(1)}, u32[]{:S(2)}, u32[]{:S(2)}) collective-permute-start(f32[48,1,8,128]{3,0,2,1:T(8,128)S(1)} %get-tuple-element.77), channel_id=1, source_target_pairs={{2,0},{4,2},{6,4},{8,6},{10,8},{12,10},{14,12},{16,14},{18,16},{20... | collective-permute-start | bytes 589832 | tf_op jit(solution)/shard_map/ppermute | solution.py:19
  195.5 2.6 collective-permute-start.15
  196.8 3.3 collective-permute-start.14
  243.3 11.6 %collective-permute-start.17 = (f32[48,1,8,128]{3,0,2,1:T(8,128)S(1)}, f32[48,1,8,128]{3,0,2,1:T(8,128)S(1)}, u32[]{:S(2)}, u32[]{:S(2)}) collective-permute-start(f32[48,1,8,128]{3,0,2,1:T(8,128)S(1)} %get-tuple-element.74), channel_id=1, source_target_pairs={{0,2},{2,4},{4,6},{6,8},{8,10},{10,12},{12,14},{14,16},{16,18},{18... | collective-permute-start | bytes 589832 | tf_op jit(solution)/shard_map/ppermute | solution.py:17
  247.5 9.3 %collective-permute-start.16 = (f32[48,1,8,128]{3,0,2,1:T(8,128)S(1)}, f32[48,1,8,128]{3,0,2,1:T(8,128)S(1)}, u32[]{:S(2)}, u32[]{:S(2)}) collective-permute-start(f32[48,1,8,128]{3,0,2,1:T(8,128)S(1)} %get-tuple-element.75), channel_id=1, source_target_pairs={{2,0},{4,2},{6,4},{8,6},{10,8},{12,10},{14,12},{16,14},{18,16},{20... | collective-permute-start | bytes 589832 | tf_op jit(solution)/shard_map/ppermute | solution.py:19
  256.8 2.8 collective-permute-start.19
  258.1 3.3 collective-permute-start.18
  303.6 7.4 %collective-permute-start.21 = (f32[48,1,8,128]{3,0,2,1:T(8,128)S(1)}, f32[48,1,8,128]{3,0,2,1:T(8,128)S(1)}, u32[]{:S(2)}, u32[]{:S(2)}) collective-permute-start(f32[48,1,8,128]{3,0,2,1:T(8,128)S(1)} %get-tuple-element.72), channel_id=1, source_target_pairs={{0,2},{2,4},{4,6},{6,8},{8,10},{10,12},{12,14},{14,16},{16,18},{18... | collective-permute-start | bytes 589832 | tf_op jit(solution)/shard_map/ppermute | solution.py:17
  307.8 9.1 %collective-permute-start.20 = (f32[48,1,8,128]{3,0,2,1:T(8,128)S(1)}, f32[48,1,8,128]{3,0,2,1:T(8,128)S(1)}, u32[]{:S(2)}, u32[]{:S(2)}) collective-permute-start(f32[48,1,8,128]{3,0,2,1:T(8,128)S(1)} %get-tuple-element.73), channel_id=1, source_target_pairs={{2,0},{4,2},{6,4},{8,6},{10,8},{12,10},{14,12},{16,14},{18,16},{20... | collective-permute-start | bytes 589832 | tf_op jit(solution)/shard_map/ppermute | solution.py:19
  316.9 2.6 collective-permute-start.23
  318.2 3.3 collective-permute-start.22
  364.9 11.6 %collective-permute-start.25 = (f32[48,1,8,128]{3,0,2,1:T(8,128)S(1)}, f32[48,1,8,128]{3,0,2,1:T(8,128)S(1)}, u32[]{:S(2)}, u32[]{:S(2)}) collective-permute-start(f32[48,1,8,128]{3,0,2,1:T(8,128)S(1)} %get-tuple-element.70), channel_id=1, source_target_pairs={{0,2},{2,4},{4,6},{6,8},{8,10},{10,12},{12,14},{14,16},{16,18},{18... | collective-permute-start | bytes 589832 | tf_op jit(solution)/shard_map/ppermute | solution.py:17
  369.1 9.3 %collective-permute-start.24 = (f32[48,1,8,128]{3,0,2,1:T(8,128)S(1)}, f32[48,1,8,128]{3,0,2,1:T(8,128)S(1)}, u32[]{:S(2)}, u32[]{:S(2)}) collective-permute-start(f32[48,1,8,128]{3,0,2,1:T(8,128)S(1)} %get-tuple-element.71), channel_id=1, source_target_pairs={{2,0},{4,2},{6,4},{8,6},{10,8},{12,10},{14,12},{16,14},{18,16},{20... | collective-permute-start | bytes 589832 | tf_op jit(solution)/shard_map/ppermute | solution.py:19
  378.4 2.6 collective-permute-start.27
  379.7 3.3 collective-permute-start.26
  425.2 7.4 %collective-permute-start.29 = (f32[48,1,8,128]{3,0,2,1:T(8,128)S(1)}, f32[48,1,8,128]{3,0,2,1:T(8,128)S(1)}, u32[]{:S(2)}, u32[]{:S(2)}) collective-permute-start(f32[48,1,8,128]{3,0,2,1:T(8,128)S(1)} %get-tuple-element.68), channel_id=1, source_target_pairs={{0,2},{2,4},{4,6},{6,8},{8,10},{10,12},{12,14},{14,16},{16,18},{18... | collective-permute-start | bytes 589832 | tf_op jit(solution)/shard_map/ppermute | solution.py:17
  429.4 9.1 %collective-permute-start.28 = (f32[48,1,8,128]{3,0,2,1:T(8,128)S(1)}, f32[48,1,8,128]{3,0,2,1:T(8,128)S(1)}, u32[]{:S(2)}, u32[]{:S(2)}) collective-permute-start(f32[48,1,8,128]{3,0,2,1:T(8,128)S(1)} %get-tuple-element.69), channel_id=1, source_target_pairs={{2,0},{4,2},{6,4},{8,6},{10,8},{12,10},{14,12},{16,14},{18,16},{20... | collective-permute-start | bytes 589832 | tf_op jit(solution)/shard_map/ppermute | solution.py:19
  438.5 2.6 collective-permute-start.31
  439.8 3.3 collective-permute-start.30
  (10 other events, 309.1 us)
where the time goes:
time: 645 us; the launch traced here: 635 us
  blocking collectives  433 us (67%)
  waiting for transfers between devices  79.2 us (12%)
  starting transfers between devices  65.5 us (10%)
  other arithmetic  26.5 us (4%)
  matrix products  25 us (4%)
    psum x4, blocking collectives, shards(): lax.psum((local_dot(halfway_image, halfway), local_dot(halfway_image, hal...  157 us
    psum x4, blocking collectives, shards(): lax.psum(local_dot(shadow, search_image), ('wide', 'narrow')) / total_cells  155 us
    ppermute x16, waiting for transfers between devices, padded_2(): lax.ppermute(head, axis, [((i + 1) % count, i) for i in range(ends)])  46.5 us
    ppermute x16, starting transfers between devices, padded_2(): lax.ppermute(tail, axis, [(i, (i + 1) % count) for i in range(ends)])  44.6 us
    psum x1, blocking collectives, shards(): lax.psum(jnp.einsum('bc,kc->bk', vflat, once, precision=high), ('wide', '...  41 us
    psum x1, blocking collectives, shards(): lax.psum(jnp.einsum('bc,kc->bk', vflat, wflat, precision=high), ('wide',...  40.2 us
    psum x1, blocking collectives, shards(): lax.psum(jnp.sum(twice * twice, axis=1), ('wide', 'narrow')) / total_cells  39.6 us
    ppermute x16, waiting for transfers between devices, padded_2(): lax.ppermute(tail, axis, [(i, (i + 1) % count) for i in range(ends)])  32.8 us
  transfers between devices with their start and end apart: 32, of which 24 were waited for; matrix products, arithmetic and copies ran while one was open for 0% of the time, Pallas kernels for 0%

commit v1 on v0

v1 whole, which is shorter than its diff:
```python
import functools
import math

import jax
import jax.numpy as jnp
from jax import lax
from jax.experimental import pallas as pl
from jax.experimental.pallas import tpu as pltpu
from jax.sharding import PartitionSpec as P

ITERS = 4
AXES = ("wide", "narrow")
SUB, LANE = 8, 128


def spread(coef):
    return coef[:, None, None, None]


def reduced(partial):
    count = lax.axis_size(AXES)
    copies = jnp.broadcast_to(partial[None], (count,) + partial.shape)
    return jnp.sum(lax.all_to_all(copies, AXES, 0, 0), axis=0)


def reduced_rows(partial):
    count = lax.axis_size(AXES)
    rows = partial.shape[0]
    share = partial.reshape((count, rows // count) + partial.shape[1:])
    own = jnp.sum(lax.all_to_all(share, AXES, 0, 0), axis=0)
    copies = jnp.broadcast_to(own[None], (count,) + own.shape)
    return lax.all_to_all(copies, AXES, 0, 0).reshape(partial.shape)


def padded_2(cells, sides):
    for axis, dim in sides:
        count = lax.axis_size(axis)
        ends = count - 1
        head = lax.slice_in_dim(cells, 0, 1, axis=dim)
        tail = lax.slice_in_dim(cells, cells.shape[dim] - 1, cells.shape[dim], axis=dim)
        cells = jnp.concatenate(
            [
                lax.ppermute(tail, axis, [(i, (i + 1) % count) for i in range(ends)]),
                cells,
                lax.ppermute(head, axis, [((i + 1) % count, i) for i in range(ends)]),
            ],
            axis=dim,
        )
    return cells


def operate(values, conductance, shift_col):
    padded = padded_2(values, (("wide", 1), ("narrow", 2)))
    center = padded[:, 1:-1, 1:-1, :]
    deeper = jnp.pad(padded, ((0, 0), (0, 0), (0, 0), (1, 1)))
    beside_all = deeper[:, 2:, 1:-1, 1:-1] + deeper[:, :-2, 1:-1, 1:-1]
    beside_all = beside_all + deeper[:, 1:-1, 2:, 1:-1] + deeper[:, 1:-1, :-2, 1:-1]
    beside_all = beside_all + deeper[:, 1:-1, 1:-1, 2:] + deeper[:, 1:-1, 1:-1, :-2]
    return conductance[None] * (6.0 * center - beside_all) + spread(shift_col) * center


def local_dot(left, right):
    return jnp.sum(left * right, axis=(1, 2, 3))


def solve_spread(inputs, conductance, shifts, total_cells):
    shift_col = jnp.repeat(shifts, inputs.shape[0])
    shadow = jnp.tile(inputs, (shifts.shape[0], 1, 1, 1))
    solution = jnp.zeros_like(shadow)
    residual = shadow
    search = shadow
    rho_now = lax.psum(local_dot(shadow, shadow), AXES) / total_cells
    for iteration in range(ITERS):
        search_image = operate(search, conductance, shift_col)
        denominator = lax.psum(local_dot(shadow, search_image), AXES) / total_cells
        step_alpha = rho_now / denominator
        halfway = residual - spread(step_alpha) * search_image
        halfway_image = operate(halfway, conductance, shift_col)
        cross_sum, square_sum, shadow_half, shadow_image = lax.psum(
            (
                local_dot(halfway_image, halfway),
                local_dot(halfway_image, halfway_image),
                local_dot(shadow, halfway),
                local_dot(shadow, halfway_image),
            ),
            AXES,
        )
        step_omega = cross_sum / total_cells / (square_sum / total_cells + 1e-06)
        solution = solution + spread(step_alpha) * search + spread(step_omega) * halfway
        residual = halfway - spread(step_omega) * halfway_image
        rho_next = shadow_half / total_cells - step_omega * (shadow_image / total_cells)
        if iteration + 1 < ITERS:
            step_beta = rho_next / rho_now * (step_alpha / step_omega)
            search = residual + spread(step_beta) * (search - spread(step_omega) * search_image)
            rho_now = rho_next
    return solution.reshape(shadow.shape[0], -1)


def solve_body(shift_ref, field_ref, out_ref, *scratch, dims, slots, total_cells):
    wide, narrow, near, rows = dims
    depth = wide * near // SUB
    height = narrow * rows
    shadow, cond = scratch[0], scratch[1]
    per = scratch[2:]
    names = ("x", "r", "v", "t", "p", "s")
    col = [dict(zip(names, per[6 * a : 6 * a + 6])) for a in range(slots)]
    zero = jnp.zeros((SUB, LANE), jnp.float32)
    lane = lax.broadcasted_iota(jnp.int32, (SUB, LANE), 1)
    sub = lax.broadcasted_iota(jnp.int32, (SUB, LANE), 0)
    first_lane, last_lane = lane == 0, lane == LANE - 1
    first_sub, last_sub = sub == 0, sub == SUB - 1
    jump = depth // near * 2 * near * rows

    for half in range(narrow):
        for i in range(depth):
            for y in range(rows):
                base = (((half * wide + i // near) * 2) * near + i % near) * rows + y
                shadow[i, half * rows + y] = field_ref[pl.ds(base, SUB, stride=jump), :]
                cond[i, half * rows + y] = field_ref[pl.ds(base + near * rows, SUB, stride=jump), :]

    def edges(ref):
        for y in range(height):
            low = pltpu.roll(ref[depth, y + 1], 1, 0)
            ref[0, y + 1] = jnp.where(first_sub, 0.0, low)
            high = pltpu.roll(ref[1, y + 1], SUB - 1, 0)
            ref[depth + 1, y + 1] = jnp.where(last_sub, 0.0, high)

    def image(ref, i, y, here, c, shift):
        nb = ref[i, y + 1] + ref[i + 2, y + 1]
        nb = nb + (ref[i + 1, y] + ref[i + 1, y + 2])
        nb = nb + (
            jnp.where(first_lane, 0.0, pltpu.roll(here, 1, 1)) + jnp.where(last_lane, 0.0, pltpu.roll(here, LANE - 1, 1))
        )
        return c * (6.0 * here - nb) + shift * here

    def mean(acc):
        return jnp.sum(jnp.sum(acc, axis=0, keepdims=True), axis=1, keepdims=True) / total_cells

    def wide_of(scalar):
        return jnp.broadcast_to(scalar, (SUB, LANE))

    for a in range(slots):
        for name in ("p", "s"):
            for i in range(depth + 2):
                col[a][name][i, 0] = zero
                col[a][name][i, height + 1] = zero
    shift = [jnp.full((SUB, LANE), shift_ref[a], jnp.float32) for a in range(slots)]

    def start(i, acc):
        for y in range(height):
            b = shadow[i, y]
            acc = acc + b * b
            for a in range(slots):
                col[a]["p"][i + 1, y + 1] = b
        return acc

    rho0 = wide_of(mean(lax.fori_loop(0, depth, start, zero)))
    rho = [rho0] * slots
    for a in range(slots):
        edges(col[a]["p"])

    for it in range(ITERS):
        first, last = it == 0, it == ITERS - 1

        def phase_a(i, acc):
            acc = list(acc)
            for y in range(height):
                b, c = shadow[i, y], cond[i, y]
                for a in range(slots):
                    p = col[a]["p"]
                    v = image(p, i, y, p[i + 1, y + 1], c, shift[a])
                    col[a]["v"][i, y] = v
                    acc[a] = acc[a] + b * v
            return tuple(acc)

        acc = lax.fori_loop(0, depth, phase_a, (zero,) * slots)
        alpha = [rho[a] / wide_of(mean(acc[a])) for a in range(slots)]

        def phase_b(i, _):
            for y in range(height):
                for a in range(slots):
                    r = shadow[i, y] if first else col[a]["r"][i, y]
                    col[a]["s"][i + 1, y + 1] = r - alpha[a] * col[a]["v"][i, y]
            return 0

        lax.fori_loop(0, depth, phase_b, 0)
        for a in range(slots):
            edges(col[a]["s"])

        def phase_c(i, acc):
            acc = [list(one) for one in acc]
            for y in range(height):
                b, c = shadow[i, y], cond[i, y]
                for a in range(slots):
                    ref = col[a]["s"]
                    s = ref[i + 1, y + 1]
                    t = image(ref, i, y, s, c, shift[a])
                    col[a]["t"][i, y] = t
                    acc[a][0] = acc[a][0] + t * s
                    acc[a][1] = acc[a][1] + t * t
                    if not last:
                        acc[a][2] = acc[a][2] + b * s
                        acc[a][3] = acc[a][3] + b * t
            return tuple(tuple(one) for one in acc)

        acc = lax.fori_loop(0, depth, phase_c, ((zero,) * (2 if last else 4),) * slots)
        omega, beta = [], []
        for a in range(slots):
            means = [wide_of(mean(one)) for one in acc[a]]
            omega.append(means[0] / (means[1] + 1e-06))
            if not last:
                rho_next = means[2] - omega[a] * means[3]
                beta.append(rho_next / rho[a] * (alpha[a] / omega[a]))
                rho[a] = rho_next

        def phase_d(i, _):
            for y in range(height):
                for a in range(slots):
                    p, s = col[a]["p"][i + 1, y + 1], col[a]["s"][i + 1, y + 1]
                    x = alpha[a] * p + omega[a] * s
                    if not first:
                        x = col[a]["x"][i, y] + x
                    col[a]["x"][i, y] = x
                    if not last:
                        r = s - omega[a] * col[a]["t"][i, y]
                        col[a]["r"][i, y] = r
                        col[a]["p"][i + 1, y + 1] = r + beta[a] * (p - omega[a] * col[a]["v"][i, y])
            return 0

        lax.fori_loop(0, depth, phase_d, 0)
        if not last:
            for a in range(slots):
                edges(col[a]["p"])

    for half in range(narrow):
        for a in range(slots):
            for i in range(depth):
                for y in range(rows):
                    base = ((half * slots + a) * depth * SUB + i) * rows + y
                    out_ref[pl.ds(base, SUB, stride=depth * rows), :] = col[a]["x"][i, half * rows + y]


def solve_whole(inputs, conductance, shifts, total_cells):
    wide, narrow = lax.axis_size("wide"), lax.axis_size("narrow")
    columns, near, rows, lanes = inputs.shape
    count = shifts.shape[0]
    slots = -(-count // narrow)
    sent = jnp.stack([inputs, jnp.broadcast_to(conductance[None], inputs.shape)], axis=1)
    got = lax.all_to_all(sent, "wide", 0, 0)
    fields = lax.all_gather(got, "narrow", axis=0)
    mine = lax.axis_index("narrow") * slots + jnp.arange(slots)
    own_shifts = shifts[jnp.minimum(mine, count - 1)]
    planes, height = wide * near, narrow * rows
    depth = planes // SUB
    plain = pltpu.VMEM((depth, height, SUB, LANE), jnp.float32)
    ringed = pltpu.VMEM((depth + 2, height + 2, SUB, LANE), jnp.float32)
    x = pl.pallas_call(
        functools.partial(solve_body, dims=(wide, narrow, near, rows), slots=slots, total_cells=total_cells),
        out_shape=jax.ShapeDtypeStruct((narrow * slots * planes * rows, LANE), jnp.float32),
        in_specs=[pl.BlockSpec(memory_space=pltpu.SMEM), pl.BlockSpec(memory_space=pltpu.VMEM)],
        out_specs=pl.BlockSpec(memory_space=pltpu.VMEM),
        scratch_shapes=[plain, plain] + [plain, plain, plain, plain, ringed, ringed] * slots,
        name="solve_whole",
    )(own_shifts, fields.reshape(-1, LANE))
    x = x.reshape(narrow, slots, wide, near * rows * lanes)
    x = lax.all_to_all(x, "narrow", 0, 0)
    x = x.reshape(narrow * slots, wide, -1)[:count]
    return lax.all_to_all(x.transpose(1, 0, 2), "wide", 0, 0)


def fits_whole(inputs, shifts):
    wide, narrow = lax.axis_size("wide"), lax.axis_size("narrow")
    columns, near, rows, lanes = inputs.shape
    slots = -(-shifts.shape[0] // narrow)
    field = wide * narrow * near * rows * lanes * 4
    return (
        columns == wide
        and lanes == LANE
        and wide % SUB == 0
        and rows % SUB == 0
        and field * (8 + 8 * slots) <= 24 * 2**20
    )


def shards(inputs, old_basis, conductance, shifts):
    total_cells = math.prod(inputs.shape[1:]) * lax.axis_size(AXES)
    columns, count = inputs.shape[0], shifts.shape[0]
    vflat = old_basis.reshape(old_basis.shape[0], -1)
    high = lax.Precision.HIGHEST
    gram = jnp.einsum("bc,dc->bd", vflat, vflat, precision=high)
    whole = fits_whole(inputs, shifts)
    if whole:
        wflat = solve_whole(inputs, conductance, shifts, total_cells).reshape(columns * count, -1)
    else:
        wflat = solve_spread(inputs, conductance, shifts, total_cells)
    first = jnp.einsum("bc,kc->bk", vflat, wflat, precision=high)
    if old_basis.shape[0] % lax.axis_size(AXES) == 0:
        both = reduced_rows(jnp.concatenate([first, gram], axis=1))
    else:
        both = lax.psum(jnp.concatenate([first, gram], axis=1), AXES)
    both = both / total_cells
    first, gram = both[:, : columns * count], both[:, columns * count :]
    coef = first + (first - jnp.matmul(gram, first, precision=high))
    twice = wflat - jnp.einsum("bk,bc->kc", coef, vflat, precision=high)
    mean_square = reduced(jnp.sum(twice * twice, axis=1)) / total_cells
    col_scale = jnp.sqrt(mean_square + 1e-06)
    new_columns = twice / col_scale[:, None]
    if whole:
        new_columns = new_columns.reshape(columns, count, -1).transpose(1, 0, 2)
        coef = coef.reshape(-1, columns, count).transpose(0, 2, 1).reshape(-1, columns * count)
        col_scale = col_scale.reshape(columns, count).T.reshape(-1)
    return (new_columns.reshape((columns * count,) + inputs.shape[1:]), coef, col_scale)


def solution(mesh):
    in_specs = (
        P(None, "wide", "narrow", None),
        P(None, "wide", "narrow", None),
        P("wide", "narrow", None),
        P(),
    )
    out_specs = (P(None, "wide", "narrow", None), P(), P())
    return jax.shard_map(shards, mesh=mesh, in_specs=in_specs, out_specs=out_specs, check_vma=False)
```

time: 645 us -> 165 us (0.26); the launches traced: 635 us -> 164 us
  blocking collectives: 433 us -> 61.7 us
  waiting for transfers between devices: 79.2 us -> 20.1 us
  starting transfers between devices: 65.5 us -> 9.39 us
  other arithmetic: 26.5 us -> 1.29 us
  Pallas kernels: 0 us -> 16.1 us
  between operations: 1.79 us -> 14.2 us
  matrix products: 25 us -> 32.3 us
    psum x11 -> x0, blocking collectives: 433 us -> none  [the longest x4 157 us: shards(): lax.psum((local_dot(halfway_image, halfway), local_dot(halfway_image, hal...]
    ppermute x32 -> x0, waiting for transfers between devices: 79.2 us -> none  [the longest x16 46.5 us: padded_2(): lax.ppermute(head, axis, [((i + 1) % count, i) for i in range(ends)])]
    ppermute x32 -> x0, starting transfers between devices: 65.5 us -> none  [the longest x16 44.6 us: padded_2(): lax.ppermute(tail, axis, [(i, (i + 1) % count) for i in range(ends)])]
    all_to_all x0 -> x4, blocking collectives: none -> 61.7 us  [the longest x1 23.3 us: solve_whole(): got = lax.all_to_all(sent, 'wide', 0, 0)]
    pallas_call x0 -> x1, Pallas kernels: none -> 16.1 us  [solve_whole(): pl.pallas_call(functools.partial(solve_body, dims=(wide, narrow, near, ro...]
    all_to_all x0 -> x2, waiting for transfers between devices: none -> 13.8 us  [the longest x1 7.34 us: solve_whole(): return lax.all_to_all(x.transpose(1, 0, 2), 'wide', 0, 0)]
    all_to_all x0 -> x2, starting transfers between devices: none -> 9.35 us  [the longest x1 6.8 us: solve_whole(): return lax.all_to_all(x.transpose(1, 0, 2), 'wide', 0, 0)]
    reduce_sum x9 -> x2, other arithmetic: 8.65 us -> 0.06 us  [the longest x1 0.04 us: reduced_rows(): own = jnp.sum(lax.all_to_all(share, AXES, 0, 0), axis=0)]
  transfers between devices with their start and end apart: 32 -> 3, of which waited for: 24 -> 3; matrix products, arithmetic and copies ran while one was open for 0% -> 12% of each run, Pallas kernels for 0% -> 0%
where the time goes in v1:
time: 165 us; the launch traced here: 164 us
  blocking collectives  61.7 us (37%)
  matrix products  32.3 us (20%)
  waiting for transfers between devices  20.1 us (12%)
  Pallas kernels  16.1 us (10%)
  between operations  14.2 us (9%)
  local copies, waits for them, and re-layouts  9.4 us (6%)
  starting transfers between devices  9.39 us (6%)
    all_to_all x1, blocking collectives, solve_whole(): got = lax.all_to_all(sent, 'wide', 0, 0)  23.3 us
    all_to_all x1, blocking collectives, reduced_rows(): own = jnp.sum(lax.all_to_all(share, AXES, 0, 0), axis=0)  18.2 us
    dot_general x1, matrix products, shards(): gram = jnp.einsum('bc,dc->bd', vflat, vflat, precision=high)  17.2 us
    pallas_call x1, Pallas kernels, solve_whole(): pl.pallas_call(functools.partial(solve_body, dims=(wide, narrow, near, ro...  16.1 us
    all_to_all x1, blocking collectives, reduced_rows(): return lax.all_to_all(copies, AXES, 0, 0).reshape(partial.shape)  15.6 us
    dot_general x1, matrix products, shards(): first = jnp.einsum('bc,kc->bk', vflat, wflat, precision=high)  7.53 us
    all_to_all x1, waiting for transfers between devices, solve_whole(): return lax.all_to_all(x.transpose(1, 0, 2), 'wide', 0, 0)  7.34 us
    dot_general x1, matrix products, shards(): twice = wflat - jnp.einsum('bk,bc->kc', coef, vflat, precision=high)  7.05 us
  transfers between devices with their start and end apart: 3, of which 3 were waited for; matrix products, arithmetic and copies ran while one was open for 12% of the time, Pallas kernels for 0%

profile of v1, /device:TPU:0, one launch (start us, length us, event | category | flops | bytes accessed | tf_op | source)
XLA Modules:
  0.0 164.4 jit_solution(3228197320301247519)
XLA Ops:
  7.2 0.7 stack_broadcast_in_dim.2
  8.0 1.0 pad_maximum_fusion
  9.0 23.3 %all_to_all.31 = f32[16,2,4,8,128]{4,3,2,1,0:T(8,128)} all-to-all(f32[16,2,4,8,128]{4,3,2,1,0:T(8,128)S(1)} %pad_maximum_fusion), channel_id=1, replica_groups=mesh['wide'=16,'narrow'=2] {'wide'}, dimensions={0} | all-to-all | bytes 1048576 | tf_op jit(solution)/shard_map/all_to_all | solution.py:249
  32.4 1.1 gather_fusion
  33.5 6.3 %all-gather.3.cloned.1.call-done = f32[32,2,4,8,128]{4,3,2,1,0:T(8,128)} async-done(((f32[16,2,4,8,128]{4,3,2,1,0:T(8,128)}), f32[32,2,4,8,128]{4,3,2,1,0:T(8,128)}) %all-gather.3.cloned.1.call-update) | async-done | bytes 1048592 | tf_op jit(solution)/shard_map/all_gather | solution.py:250
  39.9 16.1 %solve_whole.1 = f32[2048,128]{1,0:T(8,128)} custom-call(f32[2]{0:T(128)} %gather_fusion, f32[2048,128]{1,0:T(8,128)} %bitcast.47), custom_call_target="tpu_custom_call" | custom-call | tf_op jit(solution)/shard_map/solve_whole/pallas_call | solution.py:257
  55.9 1.4 reshape.81
  57.3 4.6 %all_to_all.32 = f32[2,2,16,4096]{3,2,1,0:T(8,128)S(1)} all-to-all(f32[2,2,16,4096]{3,2,1,0:T(8,128)S(1)} %reshape.81), channel_id=1, replica_groups=mesh['wide'=16,'narrow'=2] {'narrow'}, dimensions={0} | all-to-all | bytes 2097152 | tf_op jit(solution)/shard_map/all_to_all | solution.py:266
  61.9 0.1 slice.14
  62.0 1.5 copy.86
  63.5 6.8 %all-to-all-start.2 = ((f32[16,3,4096]{2,1,0:T(4,128)}), f32[16,3,4096]{2,1,0:T(4,128)S(1)}, u32[]{:S(2)}, u32[]{:S(2)}) async-start(f32[16,3,4096]{2,1,0:T(4,128)} %bitcast.40), calls=%async_computation.2 | async-start | bytes 2097152 | tf_op jit(solution)/shard_map/all_to_all | solution.py:268
  70.3 17.2 %fusion.7 = f32[256,256]{0,1:T(8,128)S(1)} fusion(f32[256,4,8,128]{3,2,1,0:T(8,128)} %param.5), kind=kOutput, calls=%fused_computation.9 | convolution fusion | flops 3221225472 | bytes 4456448 | tf_op jit(solution)/shard_map/bc,dc->bd/dot_general | solution.py:290
  87.5 7.3 %all-to-all-done.2 = f32[16,3,4096]{2,1,0:T(4,128)S(1)} async-done(((f32[16,3,4096]{2,1,0:T(4,128)}), f32[16,3,4096]{2,1,0:T(4,128)S(1)}, u32[]{:S(2)}, u32[]{:S(2)}) %all-to-all-start.2) | async-done | bytes 786464 | tf_op jit(solution)/shard_map/all_to_all | solution.py:268
  94.9 0.4 reshape.83
  95.3 7.5 %fusion.10 = f32[256,48]{0,1:T(8,128)S(1)} fusion(f32[48,4096]{1,0:T(8,128)S(1)} %reshape.83, f32[32,8,32,128]{3,2,1,0:T(8,128)} %bitcast.41), kind=kOutput, calls=%fused_computation.10 | convolution fusion | flops 603979776 | bytes 5029888 | tf_op jit(solution)/shard_map/bc,kc->bk/dot_general | solution.py:296
  102.9 0.2 copy.57
  103.0 18.2 %all_to_all.33 = f32[32,8,304]{2,1,0:T(8,128)S(1)} all-to-all(f32[32,8,304]{2,1,0:T(8,128)S(1)} %bitcast.46), channel_id=1, replica_groups=mesh['wide'=16,'narrow'=2] {'wide','narrow'}, dimensions={0} | all-to-all | bytes 622592 | tf_op jit(solution)/shard_map/all_to_all | solution.py:30
  121.3 15.6 %all_to_all.34 = f32[32,8,304]{2,1,0:T(8,128)S(1)} all-to-all(f32[32,8,304]{2,1,0:T(8,128)S(1)} %broadcast_in_dim.4), channel_id=1, replica_groups=mesh['wide'=16,'narrow'=2] {'wide','narrow'}, dimensions={0} | all-to-all | bytes 622592 | tf_op jit(solution)/shard_map/all_to_all | solution.py:32
  136.9 0.1 copy.66
  137.0 0.5 fusion.13
  137.5 7.1 %multiply_reduce_fusion = (f32[48]{0:T(128)S(1)}, f32[48,4096]{1,0:T(8,128)S(1)}) fusion(f32[48,4096]{1,0:T(8,128)S(1)} %reshape.83, f32[256,48]{0,1:T(8,128)S(1)} %fusion.13, f32[32,8,32,128]{3,2,1,0:T(8,128)} %bitcast.42), kind=kOutput, calls=%fused_computation.14 | convolution fusion | flops 604569536 | bytes 5816512 | tf_op jit(solution)/shard_map/bk,bc->kc/dot_general | solution.py:304
  144.5 0.6 broadcast_in_dim.5
  145.1 2.5 %all-to-all-start.5 = ((f32[32,1,48]{2,1,0:T(1,128)}), f32[32,1,48]{2,1,0:T(1,128)S(1)}, u32[]{:S(2)}, u32[]{:S(2)}) async-start(f32[32,1,48]{2,1,0:T(1,128)} %broadcast_in_dim.5), calls=%async_computation.5 | async-start | bytes 32768 | tf_op jit(solution)/shard_map/all_to_all | solution.py:23
  147.7 0.6 copy.61
  148.4 6.4 %all-to-all-done.5 = f32[32,1,48]{2,1,0:T(1,128)S(1)} async-done(((f32[32,1,48]{2,1,0:T(1,128)}), f32[32,1,48]{2,1,0:T(1,128)S(1)}, u32[]{:S(2)}, u32[]{:S(2)}) %all-to-all-start.5) | async-done | bytes 6176 | tf_op jit(solution)/shard_map/all_to_all | solution.py:23
  154.8 0.1 sqrt.12
  154.9 0.1 broadcast_divide_fusion
  155.1 0.1 copy.62
  155.1 0.6 reshape.90
  155.7 0.3 reshape.86
  156.1 0.5 copy.60
  156.5 1.0 copy.68
  (14 shorter events, 0.3 us)
Async XLA Ops:
  7.2 25.2 %copy-start = (f32[3]{0:T(128)S(1)}, f32[3]{0:T(128)}, u32[]{:S(2)}) copy-start(f32[3]{0:T(128)} %param.7) | copy-start | bytes 40
  7.2 32.7 %all-gather.3.cloned.1.call-start = ((), (), s32[]{:S(2)}) async-start(), calls=%async_computation.6 | async-start | bytes 1572864 | tf_op jit(solution)/shard_map/all_gather | solution.py:250
  63.5 31.4 %all-to-all-start.2 = ((f32[16,3,4096]{2,1,0:T(4,128)}), f32[16,3,4096]{2,1,0:T(4,128)S(1)}, u32[]{:S(2)}, u32[]{:S(2)}) async-start(f32[16,3,4096]{2,1,0:T(4,128)} %bitcast.40), calls=%async_computation.2 | async-start | bytes 2097152 | tf_op jit(solution)/shard_map/all_to_all | solution.py:268
  145.1 9.7 %all-to-all-start.5 = ((f32[32,1,48]{2,1,0:T(1,128)}), f32[32,1,48]{2,1,0:T(1,128)S(1)}, u32[]{:S(2)}, u32[]{:S(2)}) async-start(f32[32,1,48]{2,1,0:T(1,128)} %broadcast_in_dim.5), calls=%async_computation.5 | async-start | bytes 32768 | tf_op jit(solution)/shard_map/all_to_all | solution.py:23
Sparse Core Ops, SparseCore 0:
  32.5 7.3 all-gather.2

commit v2 on v1

--- a/solution.py
+++ b/solution.py
@@ -96,27 +96,35 @@
     return solution.reshape(shadow.shape[0], -1)
 
 
-def solve_body(shift_ref, field_ref, out_ref, *scratch, dims, slots, total_cells):
+def split_columns(count, narrow):
+    return count // narrow, count % narrow
+
+
+def solve_body(core_ref, shift_ref, *refs, dims, count, total_cells):
     wide, narrow, near, rows = dims
+    own, left = split_columns(count, narrow)
+    slots = own + left
     depth = wide * near // SUB
     height = narrow * rows
-    shadow, cond = scratch[0], scratch[1]
-    per = scratch[2:]
+    parts, out_ref, (shadow, cond), per = refs[:narrow], refs[narrow], refs[narrow + 1 : narrow + 3], refs[narrow + 3 :]
     names = ("x", "r", "v", "t", "p", "s")
     col = [dict(zip(names, per[6 * a : 6 * a + 6])) for a in range(slots)]
+    core = core_ref[0]
     zero = jnp.zeros((SUB, LANE), jnp.float32)
     lane = lax.broadcasted_iota(jnp.int32, (SUB, LANE), 1)
     sub = lax.broadcasted_iota(jnp.int32, (SUB, LANE), 0)
     first_lane, last_lane = lane == 0, lane == LANE - 1
     first_sub, last_sub = sub == 0, sub == SUB - 1
-    jump = depth // near * 2 * near * rows
-
-    for half in range(narrow):
+    apart = depth // near
+
+    for step in range(narrow):
+        at = lax.rem(core + step, narrow) * rows
         for i in range(depth):
             for y in range(rows):
-                base = (((half * wide + i // near) * 2) * near + i % near) * rows + y
-                shadow[i, half * rows + y] = field_ref[pl.ds(base, SUB, stride=jump), :]
-                cond[i, half * rows + y] = field_ref[pl.ds(base + near * rows, SUB, stride=jump), :]
+                base = ((i // near * 2) * near + i % near) * rows + y
+                jump = apart * 2 * near * rows
+                shadow[i, at + y] = parts[step][pl.ds(base, SUB, stride=jump), :]
+                cond[i, at + y] = parts[step][pl.ds(base + near * rows, SUB, stride=jump), :]
 
     def edges(ref):
         for y in range(height):
@@ -144,7 +152,8 @@
             for i in range(depth + 2):
                 col[a][name][i, 0] = zero
                 col[a][name][i, height + 1] = zero
-    shift = [jnp.full((SUB, LANE), shift_ref[a], jnp.float32) for a in range(slots)]
+    which = [core * own + a for a in range(own)] + [narrow * own + a for a in range(left)]
+    shift = [jnp.full((SUB, LANE), shift_ref[j], jnp.float32) for j in which]
 
     def start(i, acc):
         for y in range(height):
@@ -232,84 +241,109 @@
             for a in range(slots):
                 edges(col[a]["p"])
 
-    for half in range(narrow):
-        for a in range(slots):
-            for i in range(depth):
-                for y in range(rows):
-                    base = ((half * slots + a) * depth * SUB + i) * rows + y
-                    out_ref[pl.ds(base, SUB, stride=depth * rows), :] = col[a]["x"][i, half * rows + y]
+    share = near // narrow
+    chunk = own * near + left * share
+    jump = apart * narrow * chunk * rows
+    for to in range(narrow):
+        for group in range(apart):
+            for y in range(rows):
+                base = ((group * narrow + to) * chunk) * rows + y
+                for a in range(own):
+                    for xl in range(near):
+                        at = base + (a * near + xl) * rows
+                        out_ref[pl.ds(at, SUB, stride=jump), :] = col[a]["x"][group * near + xl, to * rows + y]
+                for e in range(left):
+                    for xl in range(share):
+                        at = base + (own * near + e * share + xl) * rows
+                        from_i = group * near + core * share + xl
+                        out_ref[pl.ds(at, SUB, stride=jump), :] = col[own + e]["x"][from_i, to * rows + y]
 
 
 def solve_whole(inputs, conductance, shifts, total_cells):
     wide, narrow = lax.axis_size("wide"), lax.axis_size("narrow")
     columns, near, rows, lanes = inputs.shape
     count = shifts.shape[0]
-    slots = -(-count // narrow)
+    own, left = split_columns(count, narrow)
+    slots = own + left
     sent = jnp.stack([inputs, jnp.broadcast_to(conductance[None], inputs.shape)], axis=1)
-    got = lax.all_to_all(sent, "wide", 0, 0)
-    fields = lax.all_gather(got, "narrow", axis=0)
-    mine = lax.axis_index("narrow") * slots + jnp.arange(slots)
-    own_shifts = shifts[jnp.minimum(mine, count - 1)]
+    got = lax.all_to_all(sent, "wide", 0, 0).reshape(-1, LANE)
+    parts = [got]
+    for step in range(1, narrow):
+        parts.append(lax.ppermute(got, "narrow", [((i + step) % narrow, i) for i in range(narrow)]))
     planes, height = wide * near, narrow * rows
     depth = planes // SUB
     plain = pltpu.VMEM((depth, height, SUB, LANE), jnp.float32)
     ringed = pltpu.VMEM((depth + 2, height + 2, SUB, LANE), jnp.float32)
+    share = near // narrow
+    chunk = own * near + left * share
+    smem, vmem = pl.BlockSpec(memory_space=pltpu.SMEM), pl.BlockSpec(memory_space=pltpu.VMEM)
     x = pl.pallas_call(
-        functools.partial(solve_body, dims=(wide, narrow, near, rows), slots=slots, total_cells=total_cells),
-        out_shape=jax.ShapeDtypeStruct((narrow * slots * planes * rows, LANE), jnp.float32),
-        in_specs=[pl.BlockSpec(memory_space=pltpu.SMEM), pl.BlockSpec(memory_space=pltpu.VMEM)],
-        out_specs=pl.BlockSpec(memory_space=pltpu.VMEM),
+        functools.partial(solve_body, dims=(wide, narrow, near, rows), count=count, total_cells=total_cells),
+        out_shape=jax.ShapeDtypeStruct((wide * narrow * chunk * rows, LANE), jnp.float32),
+        in_specs=[smem, smem] + [vmem] * narrow,
+        out_specs=vmem,
         scratch_shapes=[plain, plain] + [plain, plain, plain, plain, ringed, ringed] * slots,
         name="solve_whole",
-    )(own_shifts, fields.reshape(-1, LANE))
-    x = x.reshape(narrow, slots, wide, near * rows * lanes)
-    x = lax.all_to_all(x, "narrow", 0, 0)
-    x = x.reshape(narrow * slots, wide, -1)[:count]
-    return lax.all_to_all(x.transpose(1, 0, 2), "wide", 0, 0)
+    )(lax.axis_index("narrow").reshape(1), shifts, *parts)
+    x = lax.all_to_all(x.reshape(wide * narrow, chunk, rows, LANE), AXES, 0, 0)
+    x = x.reshape(wide, narrow, chunk, rows * lanes)
+    full = x[:, :, : own * near].reshape(wide, narrow * own, near * rows * lanes)
+    rest = x[:, :, own * near :].reshape(wide, narrow, left, share, rows * lanes).transpose(0, 2, 1, 3, 4)
+    return jnp.concatenate([full, rest.reshape(wide, left, near * rows * lanes)], axis=1)
 
 
 def fits_whole(inputs, shifts):
     wide, narrow = lax.axis_size("wide"), lax.axis_size("narrow")
     columns, near, rows, lanes = inputs.shape
-    slots = -(-shifts.shape[0] // narrow)
+    own, left = split_columns(shifts.shape[0], narrow)
     field = wide * narrow * near * rows * lanes * 4
     return (
         columns == wide
         and lanes == LANE
         and wide % SUB == 0
         and rows % SUB == 0
-        and field * (8 + 8 * slots) <= 24 * 2**20
+        and near % narrow == 0
+        and field * (6 + 8 * (own + left)) <= 24 * 2**20
     )
 
 
 def shards(inputs, old_basis, conductance, shifts):
     total_cells = math.prod(inputs.shape[1:]) * lax.axis_size(AXES)
     columns, count = inputs.shape[0], shifts.shape[0]
-    vflat = old_basis.reshape(old_basis.shape[0], -1)
+    width, basis = columns * count, old_basis.shape[0]
+    vflat = old_basis.reshape(basis, -1)
     high = lax.Precision.HIGHEST
     gram = jnp.einsum("bc,dc->bd", vflat, vflat, precision=high)
     whole = fits_whole(inputs, shifts)
     if whole:
-        wflat = solve_whole(inputs, conductance, shifts, total_cells).reshape(columns * count, -1)
+        wflat = solve_whole(inputs, conductance, shifts, total_cells).reshape(width, -1)
     else:
         wflat = solve_spread(inputs, conductance, shifts, total_cells)
     first = jnp.einsum("bc,kc->bk", vflat, wflat, precision=high)
-    if old_basis.shape[0] % lax.axis_size(AXES) == 0:
-        both = reduced_rows(jnp.concatenate([first, gram], axis=1))
+    square = jnp.sum(wflat * wflat, axis=1)
+    tall = max(basis, width)
+    square = jnp.pad(square, (0, tall - width))[:, None]
+    both = jnp.concatenate([jnp.pad(jnp.concatenate([first, gram], axis=1), ((0, tall - basis), (0, 0))), square], axis=1)
+    if tall % lax.axis_size(AXES) == 0:
+        both = reduced_rows(both)
     else:
-        both = lax.psum(jnp.concatenate([first, gram], axis=1), AXES)
+        both = lax.psum(both, AXES)
     both = both / total_cells
-    first, gram = both[:, : columns * count], both[:, columns * count :]
+    first, gram, square = both[:basis, :width], both[:basis, width:-1], both[:width, -1]
     coef = first + (first - jnp.matmul(gram, first, precision=high))
     twice = wflat - jnp.einsum("bk,bc->kc", coef, vflat, precision=high)
-    mean_square = reduced(jnp.sum(twice * twice, axis=1)) / total_cells
+    crossed = 2.0 * jnp.sum(coef * first, axis=0)
+    folded = jnp.sum(coef * jnp.matmul(gram, coef, precision=high), axis=0)
+    quick = square - crossed + folded
+    safe = jnp.all(quick >= 0.1 * (square + jnp.abs(crossed) + folded))
+    mean_square = lax.cond(safe, lambda: quick, lambda: reduced(jnp.sum(twice * twice, axis=1)) / total_cells)
     col_scale = jnp.sqrt(mean_square + 1e-06)
     new_columns = twice / col_scale[:, None]
     if whole:
         new_columns = new_columns.reshape(columns, count, -1).transpose(1, 0, 2)
-        coef = coef.reshape(-1, columns, count).transpose(0, 2, 1).reshape(-1, columns * count)
+        coef = coef.reshape(-1, columns, count).transpose(0, 2, 1).reshape(-1, width)
         col_scale = col_scale.reshape(columns, count).T.reshape(-1)
-    return (new_columns.reshape((columns * count,) + inputs.shape[1:]), coef, col_scale)
+    return (new_columns.reshape((width,) + inputs.shape[1:]), coef, col_scale)
 
 
 def solution(mesh):

time: 165 us -> 125 us (0.76)
  waiting for transfers between devices: 20.1 us -> 5.37 us
  between operations: 14.2 us -> 1.51 us
  starting transfers between devices: 9.39 us -> 2.93 us
  blocking collectives: 61.7 us -> 55.5 us
    all_to_all x2 -> x1, waiting for transfers between devices: 13.8 us -> 3.47 us  [solve_whole(): x = lax.all_to_all(x.reshape(wide * narrow, chunk, rows, LANE), AXES, 0, 0)]
    all_to_all x2 -> x1, starting transfers between devices: 9.35 us -> 2.93 us  [solve_whole(): x = lax.all_to_all(x.reshape(wide * narrow, chunk, rows, LANE), AXES, 0, 0)]
    all_gather x1 -> x0, waiting for transfers between devices: 6.33 us -> none  [solve_whole(): fields = lax.all_gather(got, 'narrow', axis=0)]
    all_to_all x2 -> x1, blocking collectives: 27.9 us -> 23.2 us  [solve_whole(): got = lax.all_to_all(sent, 'wide', 0, 0).reshape(-1, LANE)]
    ppermute x0 -> x1, waiting for transfers between devices: none -> 1.91 us  [solve_whole(): lax.ppermute(got, 'narrow', [((i + step) % narrow, i) for i in range(narr...]
  transfers between devices with their start and end apart: 3 -> 2, of which waited for: 3 -> 2; matrix products, arithmetic and copies ran while one was open for 12% -> 14% of each run, Pallas kernels for 0% -> 0%
where the time goes in v2:
time: 125 us; the launch traced here: 124 us
  blocking collectives  55.5 us (44%)
  matrix products  32.6 us (26%)
  Pallas kernels  15.8 us (13%)
  local copies, waits for them, and re-layouts  8.19 us (7%)
  waiting for transfers between devices  5.37 us (4%)
  starting transfers between devices  2.93 us (2%)
  other arithmetic  2.19 us (2%)
  between operations  1.51 us (1%)
    all_to_all x1, blocking collectives, solve_whole(): got = lax.all_to_all(sent, 'wide', 0, 0).reshape(-1, LANE)  23.2 us
    dot_general x1, matrix products, shards(): gram = jnp.einsum('bc,dc->bd', vflat, vflat, precision=high)  17.1 us
    all_to_all x1, blocking collectives, reduced_rows(): own = jnp.sum(lax.all_to_all(share, AXES, 0, 0), axis=0)  16.7 us
    pallas_call x1, Pallas kernels, solve_whole(): pl.pallas_call(functools.partial(solve_body, dims=(wide, narrow, near, ro...  15.8 us
    all_to_all x1, blocking collectives, reduced_rows(): return lax.all_to_all(copies, AXES, 0, 0).reshape(partial.shape)  15.6 us
    dot_general x1, matrix products, shards(): first = jnp.einsum('bc,kc->bk', vflat, wflat, precision=high)  7.51 us
    dot_general x1, matrix products, shards(): twice = wflat - jnp.einsum('bk,bc->kc', coef, vflat, precision=high)  6.92 us
    all_to_all x1, waiting for transfers between devices, solve_whole(): x = lax.all_to_all(x.reshape(wide * narrow, chunk, rows, LANE), AXES, 0, 0)  3.47 us
  transfers between devices with their start and end apart: 2, of which 2 were waited for; matrix products, arithmetic and copies ran while one was open for 14% of the time, Pallas kernels for 0%

profile of v2, /device:TPU:0, one launch (start us, length us, event | category | flops | bytes accessed | tf_op | source)
XLA Modules:
  0.0 124.1 jit_solution(1327895102025550883)
XLA Ops:
  0.6 0.7 stack_broadcast_in_dim.2
  1.4 1.0 pad_maximum_fusion
  2.4 23.2 %all_to_all.26 = f32[16,2,4,8,128]{4,3,2,1,0:T(8,128)S(1)} all-to-all(f32[16,2,4,8,128]{4,3,2,1,0:T(8,128)S(1)} %pad_maximum_fusion), channel_id=1, replica_groups=mesh['wide'=16,'narrow'=2] {'wide'}, dimensions={0} | all-to-all | bytes 1048576 | tf_op jit(solution)/shard_map/all_to_all | solution.py:269
  25.6 1.9 %collective-permute-done.refs_1_ = f32[1024,128]{1,0:T(8,128)S(1)} collective-permute-done((f32[1024,128]{1,0:T(8,128)S(1)}, f32[1024,128]{1,0:T(8,128)S(1)}, u32[]{:S(2)}, u32[]{:S(2)}) %collective-permute-start) | collective-permute-done | bytes 524320 | tf_op jit(solution)/shard_map/ppermute | solution.py:272
  27.5 0.8 copy-done.1
  28.3 15.8 %solve_whole.1 = f32[1536,128]{1,0:T(8,128)} custom-call(s32[1]{0:T(128)} %bitcast.1.core_ref, f32[3]{0:T(128)} %shift_ref.1, f32[1024,128]{1,0:T(8,128)} %bitcast.50, f32[1024,128]{1,0:T(8,128)} %copy-done.1), custom_call_target="tpu_custom_call" | custom-call | tf_op jit(solution)/shard_map/solve_whole/pallas_call | solution.py:280
  44.1 2.9 %all-to-all-start.2 = ((f32[32,6,8,128]{3,2,1,0:T(8,128)}), f32[32,6,8,128]{3,2,1,0:T(8,128)S(1)}, u32[]{:S(2)}, u32[]{:S(2)}) async-start(f32[32,6,8,128]{3,2,1,0:T(8,128)} %bitcast.48), calls=%async_computation.2 | async-start | bytes 1572864 | tf_op jit(solution)/shard_map/all_to_all | solution.py:288
  47.0 17.1 %fusion.7 = f32[32,8,256]{2,1,0:T(8,128)S(1)} fusion(f32[256,4,8,128]{3,2,1,0:T(8,128)} %param.7), kind=kOutput, calls=%fused_computation.10 | convolution fusion | flops 3221225472 | bytes 4456448 | tf_op jit(solution)/shard_map/bc,dc->bd/dot_general | solution.py:316
  64.1 3.5 %all-to-all-done.2 = f32[32,6,8,128]{3,2,1,0:T(8,128)S(1)} async-done(((f32[32,6,8,128]{3,2,1,0:T(8,128)}), f32[32,6,8,128]{3,2,1,0:T(8,128)S(1)}, u32[]{:S(2)}, u32[]{:S(2)}) %all-to-all-start.2) | async-done | bytes 786464 | tf_op jit(solution)/shard_map/all_to_all | solution.py:288
  67.7 0.4 reshape.65
  68.1 0.3 copy.63
  68.5 0.4 reshape.66
  68.9 0.2 copy.64
  69.1 0.2 reshape_transpose_reshape.3
  69.4 0.1 multiply_reduce_fusion.1
  69.5 0.6 copy.65
  70.3 0.2 concatenate.20
  70.5 0.4 reshape.67
  70.9 7.5 %fusion.10 = f32[256,48]{0,1:T(8,128)S(1)} fusion(f32[48,4096]{1,0:T(8,128)S(1)} %reshape.67, f32[32,8,32,128]{3,2,1,0:T(8,128)} %bitcast.44), kind=kOutput, calls=%fused_computation.12 | convolution fusion | flops 603979776 | bytes 5029888 | tf_op jit(solution)/shard_map/bc,kc->bk/dot_general | solution.py:322
  78.5 0.2 pad_maximum_fusion.1
  78.7 16.7 %all_to_all.27 = f32[32,8,305]{2,1,0:T(8,128)S(1)} all-to-all(f32[32,8,305]{2,1,0:T(8,128)S(1)} %pad_maximum_fusion.1), channel_id=1, replica_groups=mesh['wide'=16,'narrow'=2] {'wide','narrow'}, dimensions={0} | all-to-all | bytes 624640 | tf_op jit(solution)/shard_map/all_to_all | solution.py:30
  95.4 15.6 %all_to_all.28 = f32[32,8,305]{2,1,0:T(8,128)S(1)} all-to-all(f32[32,8,305]{2,1,0:T(8,128)S(1)} %broadcast_in_dim.4), channel_id=1, replica_groups=mesh['wide'=16,'narrow'=2] {'wide','narrow'}, dimensions={0} | all-to-all | bytes 624640 | tf_op jit(solution)/shard_map/all_to_all | solution.py:32
  111.1 0.2 slice_reduce_fusion
  111.3 0.6 multiply_reduce_fusion.2
  111.9 0.5 fusion.14
  112.4 0.6 compare_reduce_fusion
  113.1 6.9 %convolution_subtract_fusion = f32[48,4096]{1,0:T(8,128)S(1)} fusion(f32[48,4096]{1,0:T(8,128)S(1)} %reshape.67, f32[256,48]{0,1:T(8,128)S(1)} %get-tuple-element.9, f32[32,8,32,128]{3,2,1,0:T(8,128)} %bitcast.45), kind=kOutput, calls=%fused_computation.2 | convolution fusion | flops 604176384 | bytes 5816320 | tf_op jit(solution)/shard_map/bk,bc->kc/dot_general | solution.py:334
  121.0 0.6 reshape.74
  121.6 0.6 copy.73
  122.3 0.3 reshape.69
  122.6 0.5 copy.72
  123.1 1.0 copy.78
  (25 shorter events, 1.0 us)
Async XLA Ops:
  25.6 1.9 %copy-start = (f32[16,2,4,8,128]{4,3,2,1,0:T(8,128)}, f32[16,2,4,8,128]{4,3,2,1,0:T(8,128)S(1)}, u32[]{:S(2)}) copy-start(f32[16,2,4,8,128]{4,3,2,1,0:T(8,128)S(1)} %all_to_all.26) | copy-start | bytes 1572868
  25.6 1.9 %collective-permute-start = (f32[1024,128]{1,0:T(8,128)S(1)}, f32[1024,128]{1,0:T(8,128)S(1)}, u32[]{:S(2)}, u32[]{:S(2)}) collective-permute-start(f32[1024,128]{1,0:T(8,128)S(1)} %bitcast.49), channel_id=1, source_target_pairs={{1,0},{0,1},{3,2},{2,3},{5,4},{4,5},{7,6},{6,7},{9,8},{8,9},{11,10... | collective-permute-start | bytes 1572872 | tf_op jit(solution)/shard_map/ppermute | solution.py:272
  27.5 0.8 copy-start.1
  44.1 23.5 %all-to-all-start.2 = ((f32[32,6,8,128]{3,2,1,0:T(8,128)}), f32[32,6,8,128]{3,2,1,0:T(8,128)S(1)}, u32[]{:S(2)}, u32[]{:S(2)}) async-start(f32[32,6,8,128]{3,2,1,0:T(8,128)} %bitcast.48), calls=%async_computation.2 | async-start | bytes 1572864 | tf_op jit(solution)/shard_map/all_to_all | solution.py:288

commit v3 on v0

v3 whole, which is shorter than its diff:
```python
import functools
import math

import jax
import jax.numpy as jnp
from jax import lax
from jax.experimental import pallas as pl
from jax.experimental.pallas import tpu as pltpu
from jax.sharding import PartitionSpec as P

ITERS = 4
AXES = ("wide", "narrow")
SUB, LANE = 8, 128
UNROLL = 64


def spread(coef):
    return coef[:, None, None, None]


def reduced(partial):
    count = lax.axis_size(AXES)
    copies = jnp.broadcast_to(partial[None], (count,) + partial.shape)
    return jnp.sum(lax.all_to_all(copies, AXES, 0, 0), axis=0)


def reduced_rows(partial):
    count = lax.axis_size(AXES)
    share = partial.reshape((count, partial.shape[0] // count) + partial.shape[1:])
    own = jnp.sum(lax.all_to_all(share, AXES, 0, 0), axis=0)
    copies = jnp.broadcast_to(own[None], (count,) + own.shape)
    return lax.all_to_all(copies, AXES, 0, 0).reshape(partial.shape)


def padded_2(cells, sides):
    for axis, dim in sides:
        count = lax.axis_size(axis)
        ends = count - 1
        head = lax.slice_in_dim(cells, 0, 1, axis=dim)
        tail = lax.slice_in_dim(cells, cells.shape[dim] - 1, cells.shape[dim], axis=dim)
        cells = jnp.concatenate(
            [
                lax.ppermute(tail, axis, [(i, (i + 1) % count) for i in range(ends)]),
                cells,
                lax.ppermute(head, axis, [((i + 1) % count, i) for i in range(ends)]),
            ],
            axis=dim,
        )
    return cells


def operate(values, conductance, shift_col):
    padded = padded_2(values, (("wide", 1), ("narrow", 2)))
    center = padded[:, 1:-1, 1:-1, :]
    deeper = jnp.pad(padded, ((0, 0), (0, 0), (0, 0), (1, 1)))
    beside_all = deeper[:, 2:, 1:-1, 1:-1] + deeper[:, :-2, 1:-1, 1:-1]
    beside_all = beside_all + deeper[:, 1:-1, 2:, 1:-1] + deeper[:, 1:-1, :-2, 1:-1]
    beside_all = beside_all + deeper[:, 1:-1, 1:-1, 2:] + deeper[:, 1:-1, 1:-1, :-2]
    return conductance[None] * (6.0 * center - beside_all) + spread(shift_col) * center


def local_dot(left, right):
    return jnp.sum(left * right, axis=(1, 2, 3))


def solve_spread(inputs, conductance, shifts, total_cells):
    shift_col = jnp.repeat(shifts, inputs.shape[0])
    shadow = jnp.tile(inputs, (shifts.shape[0], 1, 1, 1))
    solution = jnp.zeros_like(shadow)
    residual = shadow
    search = shadow
    rho_now = lax.psum(local_dot(shadow, shadow), AXES) / total_cells
    for iteration in range(ITERS):
        search_image = operate(search, conductance, shift_col)
        denominator = lax.psum(local_dot(shadow, search_image), AXES) / total_cells
        step_alpha = rho_now / denominator
        halfway = residual - spread(step_alpha) * search_image
        halfway_image = operate(halfway, conductance, shift_col)
        cross_sum, square_sum, shadow_half, shadow_image = lax.psum(
            (
                local_dot(halfway_image, halfway),
                local_dot(halfway_image, halfway_image),
                local_dot(shadow, halfway),
                local_dot(shadow, halfway_image),
            ),
            AXES,
        )
        step_omega = cross_sum / total_cells / (square_sum / total_cells + 1e-06)
        solution = solution + spread(step_alpha) * search + spread(step_omega) * halfway
        residual = halfway - spread(step_omega) * halfway_image
        rho_next = shadow_half / total_cells - step_omega * (shadow_image / total_cells)
        if iteration + 1 < ITERS:
            step_beta = rho_next / rho_now * (step_alpha / step_omega)
            search = residual + spread(step_beta) * (search - spread(step_omega) * search_image)
            rho_now = rho_next
    return solution.reshape(shadow.shape[0], -1)


def split_columns(count, narrow):
    return count // narrow, count % narrow


def solve_body(core_ref, shift_ref, *refs, dims, count, total_cells):
    wide, narrow, near, rows = dims
    own, left = split_columns(count, narrow)
    slots = own + left
    planes, height = wide * near, narrow * rows
    parts, out_ref, (shadow, cond), per = refs[:narrow], refs[narrow], refs[narrow + 1 : narrow + 3], refs[narrow + 3 :]
    names = ("x", "r", "v", "t", "p", "s")
    col = [dict(zip(names, per[6 * a : 6 * a + 6])) for a in range(slots)]
    core = core_ref[0]
    zero = jnp.zeros((SUB, LANE), jnp.float32)
    lane = lax.broadcasted_iota(jnp.int32, (SUB, LANE), 1)
    first_lane, last_lane = lane == 0, lane == LANE - 1
    group = UNROLL
    tiles = range(0, height, SUB)

    for step in range(narrow):
        at = pl.multiple_of(lax.rem(core + step, narrow) * rows, SUB)
        shadow_half, cond_half = shadow.at[:, pl.ds(at, rows)], cond.at[:, pl.ds(at, rows)]
        for w in range(wide):
            shadow_half[w * near : (w + 1) * near] = parts[step][w, 0]
            cond_half[w * near : (w + 1) * near] = parts[step][w, 1]

    def clear(i, _):
        for a in range(slots):
            for name in ("p", "s"):
                col[a][name][i, :SUB, :] = zero
                col[a][name][i, SUB + height :, :] = zero
        return 0

    lax.fori_loop(0, planes + 2, clear, 0)
    for a in range(slots):
        for name in ("p", "s"):
            for i in (0, planes + 1):
                for y in tiles:
                    col[a][name][i, SUB + y : 2 * SUB + y, :] = zero

    def inner(ref, i, y):
        return ref[i + 1, SUB + y : 2 * SUB + y, :]

    def image(ref, i, y, here, c, shift):
        nb = ref[i, SUB + y : 2 * SUB + y, :] + ref[i + 2, SUB + y : 2 * SUB + y, :]
        nb = nb + (ref[i + 1, SUB + y - 1 : 2 * SUB + y - 1, :] + ref[i + 1, SUB + y + 1 : 2 * SUB + y + 1, :])
        nb = nb + (
            jnp.where(first_lane, 0.0, pltpu.roll(here, 1, 1)) + jnp.where(last_lane, 0.0, pltpu.roll(here, LANE - 1, 1))
        )
        return c * (6.0 * here - nb) + shift * here

    def mean(acc):
        total = jnp.sum(jnp.sum(acc, axis=1, keepdims=True), axis=0, keepdims=True) / total_cells
        return jnp.broadcast_to(total, (SUB, LANE))

    def over(body, carry):
        def some(g, carry):
            for u in range(group):
                for y in tiles:
                    carry = body(g * group + u, y, carry)
            return carry

        return lax.fori_loop(0, planes // group, some, carry)

    which = [core * own + a for a in range(own)] + [narrow * own + a for a in range(left)]
    shift = [jnp.full((SUB, LANE), shift_ref[j], jnp.float32) for j in which]

    def at_tile(ref, i, y):
        return ref[i, y : y + SUB, :]

    def start(i, y, acc):
        b = at_tile(shadow, i, y)
        for a in range(slots):
            col[a]["p"][i + 1, SUB + y : 2 * SUB + y, :] = b
            col[a]["r"][i, y : y + SUB, :] = b
            col[a]["x"][i, y : y + SUB, :] = zero
        return acc + b * b

    def half_step(rho, last):
        def phase_a(i, y, acc):
            b, c = at_tile(shadow, i, y), at_tile(cond, i, y)
            out = []
            for a in range(slots):
                p = col[a]["p"]
                v = image(p, i, y, inner(p, i, y), c, shift[a])
                col[a]["v"][i, y : y + SUB, :] = v
                out.append(acc[a] + b * v)
            return tuple(out)

        acc = over(phase_a, (zero,) * slots)
        alpha = [rho[a] / mean(acc[a]) for a in range(slots)]

        def phase_b(i, y, _):
            for a in range(slots):
                s = at_tile(col[a]["r"], i, y) - alpha[a] * at_tile(col[a]["v"], i, y)
                col[a]["s"][i + 1, SUB + y : 2 * SUB + y, :] = s
            return 0

        over(phase_b, 0)

        def phase_c(i, y, acc):
            b, c = at_tile(shadow, i, y), at_tile(cond, i, y)
            out = []
            for a in range(slots):
                ref = col[a]["s"]
                s = inner(ref, i, y)
                t = image(ref, i, y, s, c, shift[a])
                one = [acc[a][0] + t * s, acc[a][1] + t * t]
                if not last:
                    col[a]["t"][i, y : y + SUB, :] = t
                    one += [acc[a][2] + b * s, acc[a][3] + b * t]
                out.append(tuple(one))
            return tuple(out)

        acc = over(phase_c, ((zero,) * (2 if last else 4),) * slots)
        means = [[mean(one) for one in acc[a]] for a in range(slots)]
        omega = [m[0] / (m[1] + 1e-06) for m in means]
        return alpha, omega, means

    def full_step(_, rho):
        alpha, omega, means = half_step(rho, False)
        rho_next = [means[a][2] - omega[a] * means[a][3] for a in range(slots)]
        beta = [rho_next[a] / rho[a] * (alpha[a] / omega[a]) for a in range(slots)]

        def phase_d(i, y, _):
            for a in range(slots):
                p, s = inner(col[a]["p"], i, y), inner(col[a]["s"], i, y)
                col[a]["x"][i, y : y + SUB, :] = at_tile(col[a]["x"], i, y) + (alpha[a] * p + omega[a] * s)
                r = s - omega[a] * at_tile(col[a]["t"], i, y)
                col[a]["r"][i, y : y + SUB, :] = r
                next_p = r + beta[a] * (p - omega[a] * at_tile(col[a]["v"], i, y))
                col[a]["p"][i + 1, SUB + y : 2 * SUB + y, :] = next_p
            return 0

        over(phase_d, 0)
        return tuple(rho_next)

    rho0 = mean(over(start, zero))
    rho = lax.fori_loop(0, ITERS - 1, full_step, (rho0,) * slots)
    alpha, omega, _ = half_step(rho, True)

    share = near // narrow
    chunk = own * near + left * share

    def finished(a, i, y):
        p, s = inner(col[a]["p"], i, y), inner(col[a]["s"], i, y)
        return at_tile(col[a]["x"], i, y) + (alpha[a] * p + omega[a] * s)

    def send(w, _):
        for to in range(narrow):
            base = (w * narrow + to) * chunk
            for a in range(own):
                for xl in range(near):
                    out_ref[base + a * near + xl] = finished(a, w * near + xl, to * rows)
            for e in range(left):
                for xl in range(share):
                    i = w * near + core * share + xl
                    out_ref[base + own * near + e * share + xl] = finished(own + e, i, to * rows)
        return 0

    lax.fori_loop(0, wide, send, 0)


def solve_whole(inputs, conductance, shifts, total_cells, beside):
    wide, narrow = lax.axis_size("wide"), lax.axis_size("narrow")
    columns, near, rows, lanes = inputs.shape
    count = shifts.shape[0]
    own, left = split_columns(count, narrow)
    slots = own + left
    sent = jnp.stack([inputs, jnp.broadcast_to(conductance[None], inputs.shape)], axis=1)
    got = lax.all_to_all(sent, "wide", 0, 0)
    got, beside = lax.optimization_barrier((got, beside))
    parts = [got]
    for step in range(1, narrow):
        parts.append(lax.ppermute(got, "narrow", [((i + step) % narrow, i) for i in range(narrow)]))
    planes, height = wide * near, narrow * rows
    plain = pltpu.VMEM((planes, height, LANE), jnp.float32)
    ringed = pltpu.VMEM((planes + 2, height + 2 * SUB, LANE), jnp.float32)
    share = near // narrow
    chunk = own * near + left * share
    smem, vmem = pl.BlockSpec(memory_space=pltpu.SMEM), pl.BlockSpec(memory_space=pltpu.VMEM)
    x = pl.pallas_call(
        functools.partial(solve_body, dims=(wide, narrow, near, rows), count=count, total_cells=total_cells),
        out_shape=jax.ShapeDtypeStruct((wide * narrow * chunk, rows, LANE), jnp.float32),
        in_specs=[smem, smem] + [vmem] * narrow,
        out_specs=vmem,
        scratch_shapes=[plain, plain] + [plain, plain, plain, plain, ringed, ringed] * slots,
        name="solve_whole",
    )(lax.axis_index("narrow").reshape(1), shifts, *parts)
    return lax.all_to_all(x.reshape(wide * narrow, chunk, rows, LANE), AXES, 0, 0), beside


def terms(value):
    high = value.astype(jnp.bfloat16)
    rest = value - high.astype(jnp.float32)
    mid = rest.astype(jnp.bfloat16)
    return high, mid, (rest - mid.astype(jnp.float32)).astype(jnp.bfloat16)


def basis_body(source, *parts, group, held):
    for r in range(held):
        for g in range(0, group, 2 * SUB):
            low = source[pl.ds(g * held + r, SUB, stride=held), :]
            high = source[pl.ds((g + SUB) * held + r, SUB, stride=held), :]
            for part, value in zip(parts, terms(jnp.concatenate([low, high], axis=0))):
                part[g : g + 2 * SUB, r * LANE : (r + 1) * LANE] = value


def basis_terms(old_basis):
    basis = old_basis.shape[0]
    held = old_basis.shape[1] * old_basis.shape[2]
    group = 2 * SUB
    out = jax.ShapeDtypeStruct((basis, held * LANE), jnp.bfloat16)
    return pl.pallas_call(
        functools.partial(basis_body, group=group, held=held),
        grid=(basis // group,),
        out_shape=(out,) * 3,
        in_specs=[pl.BlockSpec((group * held, LANE), lambda g: (g, 0))],
        out_specs=(pl.BlockSpec((group, held * LANE), lambda g: (g, 0)),) * 3,
        name="basis_terms",
    )(old_basis.reshape(-1, LANE))


def column_row(j, xl, y, dims, count):
    wide, narrow, near, rows = dims
    own, left = split_columns(count, narrow)
    share = near // narrow
    chunk = own * near + left * share
    if j < narrow * own:
        plane = (j // own) * chunk + (j % own) * near + xl
    else:
        plane = (xl // share) * chunk + own * near + (j - narrow * own) * share + xl % share
    return plane * rows + y, narrow * chunk * rows


def layout_rows(width, basis, devices):
    blocks = basis // LANE
    used = width * blocks + LANE * blocks * (blocks + 1) // 2 + SUB
    step = devices * SUB
    return -(-used // step) * step


def block_row(width, blocks, p, q):
    return width * blocks + LANE * (p * blocks - p * (p - 1) // 2 + q - p)


def first_body(x_ref, gram, high, mid, low, out_ref, x_terms, totals, squares, *, dims, count):
    wide, narrow, near, rows = dims
    width = wide * count
    basis = high.shape[0]
    blocks = basis // LANE
    xl = pl.program_id(0)

    @pl.when(xl == 0)
    def _():
        totals[...] = jnp.zeros_like(totals)
        squares[...] = jnp.zeros_like(squares)

    for j in range(count):
        for w in range(0, wide, 2 * SUB):
            k = j * wide + w
            kept = squares[k : k + 2 * SUB, :]
            for y in range(rows):
                row, jump = column_row(j, xl, y, dims, count)
                two = [x_ref[pl.ds(row + (w + SUB * h) * jump, SUB, stride=jump), :] for h in range(2)]
                value = jnp.concatenate(two, axis=0)
                kept = kept + value * value
                for n, part in enumerate(terms(value)):
                    x_terms[n * width + k : n * width + k + 2 * SUB, y * LANE : (y + 1) * LANE] = part
            squares[k : k + 2 * SUB, :] = kept

    def against(rows_used, part):
        return lax.dot_general(
            x_terms[:rows_used, :], part[...], (((1,), (1,)), ((), ())), preferred_element_type=jnp.float32
        )

    by_high, by_mid, by_low = against(3 * width, high), against(2 * width, mid), against(width, low)
    small = (by_high[2 * width :] + by_mid[width:]) + by_low
    totals[...] += by_high[:width] + ((by_high[width : 2 * width] + by_mid[:width]) + small)

    @pl.when(xl == near - 1)
    def _():
        for p in range(blocks):
            out_ref[p * width : (p + 1) * width, :] = totals[:, p * LANE : (p + 1) * LANE]
            for q in range(p, blocks):
                at = block_row(width, blocks, p, q)
                out_ref[at : at + LANE, :] = gram[p * LANE : (p + 1) * LANE, q * LANE : (q + 1) * LANE]
        at = block_row(width, blocks, blocks - 1, blocks - 1) + LANE
        out_ref[at:, :] = jnp.zeros((out_ref.shape[0] - at, LANE), jnp.float32)
        out_ref[at : at + SUB, :] = lax.dot_general(
            jnp.ones((SUB, LANE), jnp.float32),
            squares[...],
            (((1,), (1,)), ((), ())),
            precision=lax.Precision.HIGHEST,
            preferred_element_type=jnp.float32,
        )


def first_sums(x, gram, parts, dims, count):
    wide, narrow, near, rows = dims
    width, basis = wide * count, gram.shape[0]
    vmem = pl.BlockSpec(memory_space=pltpu.VMEM)
    cells = pl.BlockSpec((basis, rows * LANE), lambda g: (0, g))
    return pl.pallas_call(
        functools.partial(first_body, dims=dims, count=count),
        grid=(near,),
        out_shape=jax.ShapeDtypeStruct((layout_rows(width, basis, wide * narrow), LANE), jnp.float32),
        in_specs=[vmem, vmem, cells, cells, cells],
        out_specs=vmem,
        scratch_shapes=[
            pltpu.VMEM((3 * width, rows * LANE), jnp.bfloat16),
            pltpu.VMEM((width, basis), jnp.float32),
            pltpu.VMEM((LANE, LANE), jnp.float32),
        ],
        name="first_sums",
    )(x, gram, *parts)


def coef_body(sums, coef_ref, terms_ref, mean_ref, bad_ref, *, width, blocks, total_cells):
    first = [sums[p * width : (p + 1) * width, :] / total_cells for p in range(blocks)]

    def gram_of(p, q):
        at = block_row(width, blocks, min(p, q), max(p, q))
        return sums[at : at + LANE, :] / total_cells

    def through(rows_of):
        out = []
        for q in range(blocks):
            total = None
            for p in range(blocks):
                side = 0 if p <= q else 1
                part = lax.dot_general(
                    rows_of[p],
                    gram_of(p, q),
                    (((1,), (side,)), ((), ())),
                    precision=lax.Precision.HIGHEST,
                    preferred_element_type=jnp.float32,
                )
                total = part if total is None else total + part
            out.append(total)
        return out

    coef = [f + (f - g) for f, g in zip(first, through(first))]
    crossed = folded = 0.0
    for p, (c, g) in enumerate(zip(coef, through(coef))):
        coef_ref[:, p * LANE : (p + 1) * LANE] = c
        for n, part in enumerate(terms(c)):
            terms_ref[n * width : (n + 1) * width, p * LANE : (p + 1) * LANE] = part
        crossed = crossed + 2.0 * jnp.sum(c * first[p], axis=1, keepdims=True)
        folded = folded + jnp.sum(c * g, axis=1, keepdims=True)
    at = block_row(width, blocks, blocks - 1, blocks - 1) + LANE
    row = jnp.broadcast_to(sums[at : at + 1, :], (width, LANE)) / total_cells
    shape = (width, LANE)
    same = lax.broadcasted_iota(jnp.int32, shape, 0) == lax.broadcasted_iota(jnp.int32, shape, 1)
    square = jnp.sum(jnp.where(same, row, 0.0), axis=1, keepdims=True)
    quick = square - crossed + folded
    fine = quick >= 0.1 * (square + jnp.abs(crossed) + folded)
    mean_ref[...] = jnp.broadcast_to(quick, shape)
    bad_ref[0] = jnp.sum(jnp.where(fine, 0.0, 1.0))


def coefficients_of(sums, width, basis, total_cells):
    vmem = pl.BlockSpec(memory_space=pltpu.VMEM)
    return pl.pallas_call(
        functools.partial(coef_body, width=width, blocks=basis // LANE, total_cells=total_cells),
        out_shape=(
            jax.ShapeDtypeStruct((width, basis), jnp.float32),
            jax.ShapeDtypeStruct((3 * width, basis), jnp.bfloat16),
            jax.ShapeDtypeStruct((width, LANE), jnp.float32),
            jax.ShapeDtypeStruct((1,), jnp.float32),
        ),
        in_specs=[vmem],
        out_specs=(vmem, vmem, vmem, pl.BlockSpec(memory_space=pltpu.SMEM)),
        name="coefficients_of",
    )(sums)


def clean_body(x_ref, coef, mean_ref, high, mid, low, out_ref, *, dims, count, scaled):
    wide, narrow, near, rows = dims
    width = wide * count
    xl = pl.program_id(0)
    flat = out_ref.reshape(width * rows, LANE)

    def against(rows_used, part):
        return lax.dot_general(
            coef[:rows_used, :], part[...], (((1,), (0,)), ((), ())), preferred_element_type=jnp.float32
        )

    by_high, by_mid, by_low = against(3 * width, high), against(2 * width, mid), against(width, low)
    small = (by_high[2 * width :] + by_mid[width:]) + by_low
    along = by_high[:width] + ((by_high[width : 2 * width] + by_mid[:width]) + small)
    for j in range(count):
        for w in range(0, wide, SUB):
            k = j * wide + w
            factor = 1.0 / jnp.sqrt(mean_ref[k : k + SUB, :] + 1e-06) if scaled else None
            for y in range(rows):
                row, jump = column_row(j, xl, y, dims, count)
                value = x_ref[pl.ds(row + w * jump, SUB, stride=jump), :]
                value = value - along[k : k + SUB, y * LANE : (y + 1) * LANE]
                if scaled:
                    value = value * factor
                flat[pl.ds(k * rows + y, SUB, stride=rows), :] = value


def cleaned(x, coef_terms, mean_square, parts, dims, count, scaled):
    wide, narrow, near, rows = dims
    width, basis = wide * count, coef_terms.shape[1]
    vmem = pl.BlockSpec(memory_space=pltpu.VMEM)
    cells = pl.BlockSpec((basis, rows * LANE), lambda g: (0, g))
    return pl.pallas_call(
        functools.partial(clean_body, dims=dims, count=count, scaled=scaled),
        grid=(near,),
        out_shape=jax.ShapeDtypeStruct((width, near * rows, LANE), jnp.float32),
        in_specs=[vmem, vmem, vmem, cells, cells, cells],
        out_specs=pl.BlockSpec((width, rows, LANE), lambda g: (0, g, 0)),
        name="cleaned",
    )(x, coef_terms, mean_square, *parts)


def shards_whole(inputs, old_basis, conductance, shifts, total_cells):
    wide, narrow = lax.axis_size("wide"), lax.axis_size("narrow")
    columns, near, rows, _ = inputs.shape
    count, basis = shifts.shape[0], old_basis.shape[0]
    width, dims = columns * count, (wide, narrow, near, rows)
    vflat = old_basis.reshape(basis, -1)
    gram = jnp.einsum("bc,dc->bd", vflat, vflat, precision=lax.Precision.HIGHEST)
    parts = basis_terms(old_basis)
    x, parts = solve_whole(inputs, conductance, shifts, total_cells, parts)
    x = x.reshape(-1, LANE)
    sums = reduced_rows(first_sums(x, gram, parts, dims, count))
    coef, coef_terms, quick, bad = coefficients_of(sums, width, basis, total_cells)

    def slow():
        twice = cleaned(x, coef_terms, quick, parts, dims, count, False)
        total = reduced(jnp.sum(twice * twice, axis=(1, 2))) / total_cells
        return jnp.broadcast_to(total[:, None], quick.shape)

    mean_square = lax.cond(bad[0] == 0.0, lambda: quick, slow)
    new_columns = cleaned(x, coef_terms, mean_square, parts, dims, count, True)
    col_scale = jnp.sqrt(mean_square[:, 0] + 1e-06)
    return (new_columns.reshape((width,) + inputs.shape[1:]), coef.T, col_scale)


def shards_spread(inputs, old_basis, conductance, shifts, total_cells):
    vflat = old_basis.reshape(old_basis.shape[0], -1)
    wflat = solve_spread(inputs, conductance, shifts, total_cells)
    high = lax.Precision.HIGHEST
    first = lax.psum(jnp.einsum("bc,kc->bk", vflat, wflat, precision=high), AXES) / total_cells
    once = wflat - jnp.einsum("bk,bc->kc", first, vflat, precision=high)
    second = lax.psum(jnp.einsum("bc,kc->bk", vflat, once, precision=high), AXES) / total_cells
    twice = once - jnp.einsum("bk,bc->kc", second, vflat, precision=high)
    mean_square = lax.psum(jnp.sum(twice * twice, axis=1), AXES) / total_cells
    col_scale = jnp.sqrt(mean_square + 1e-06)
    new_columns = (twice / col_scale[:, None]).reshape((-1,) + inputs.shape[1:])
    return (new_columns, first + second, col_scale)


def fits_whole(inputs, old_basis, shifts):
    wide, narrow = lax.axis_size("wide"), lax.axis_size("narrow")
    columns, near, rows, lanes = inputs.shape
    own, left = split_columns(shifts.shape[0], narrow)
    field = wide * narrow * near * rows * lanes * 4
    return (
        columns == wide
        and lanes == LANE
        and wide % (2 * SUB) == 0
        and rows == SUB
        and near % narrow == 0
        and wide * near % UNROLL == 0
        and old_basis.shape[0] % LANE == 0
        and columns * shifts.shape[0] <= LANE
        and field * (6 + 8 * (own + left)) <= 24 * 2**20
        and old_basis.size * 4 <= 8 * 2**20
    )


def shards(inputs, old_basis, conductance, shifts):
    total_cells = math.prod(inputs.shape[1:]) * lax.axis_size(AXES)
    form = shards_whole if fits_whole(inputs, old_basis, shifts) else shards_spread
    return form(inputs, old_basis, conductance, shifts, total_cells)


def solution(mesh):
    in_specs = (
        P(None, "wide", "narrow", None),
        P(None, "wide", "narrow", None),
        P("wide", "narrow", None),
        P(),
    )
    out_specs = (P(None, "wide", "narrow", None), P(), P())
    return jax.shard_map(shards, mesh=mesh, in_specs=in_specs, out_specs=out_specs, check_vma=False)
```

time: 645 us -> 106 us (0.16); the launches traced: 635 us -> 105 us
  blocking collectives: 433 us -> 27.2 us
  waiting for transfers between devices: 79.2 us -> 14 us
  starting transfers between devices: 65.5 us -> 11.5 us
  Pallas kernels: 0 us -> 34.6 us
  other arithmetic: 26.5 us -> 2.45 us
  matrix products: 25 us -> 12.1 us
    psum x11 -> x0, blocking collectives: 433 us -> none  [the longest x4 157 us: shards(): lax.psum((local_dot(halfway_image, halfway), local_dot(halfway_image, hal...]
    ppermute x32 -> x1, waiting for transfers between devices: 79.2 us -> 1.91 us  [solve_whole(): lax.ppermute(got, 'narrow', [((i + step) % narrow, i) for i in range(narr...]
    ppermute x32 -> x1, starting transfers between devices: 65.5 us -> 0.01 us  [solve_whole(): lax.ppermute(got, 'narrow', [((i + step) % narrow, i) for i in range(narr...]
    pallas_call x0 -> x5, Pallas kernels: none -> 34.6 us  [the longest x1 11.3 us: basis_terms(): pl.pallas_call(functools.partial(basis_body, group=group, held=held), gri...]
    all_to_all x0 -> x2, blocking collectives: none -> 27.2 us  [the longest x1 14.2 us: reduced_rows(): own = jnp.sum(lax.all_to_all(share, AXES, 0, 0), axis=0)]
    dot_general x4 -> x1, matrix products: 25 us -> 12.1 us  [shards_whole(): jnp.einsum('bc,dc->bd', vflat, vflat, precision=lax.Precision.HIGHEST)]
    all_to_all x0 -> x2, waiting for transfers between devices: none -> 12.1 us  [the longest x1 8.28 us: solve_whole(): lax.all_to_all(x.reshape(wide * narrow, chunk, rows, LANE), AXES, 0, 0)]
    all_to_all x0 -> x2, starting transfers between devices: none -> 11.5 us  [the longest x1 8.34 us: solve_whole(): got = lax.all_to_all(sent, 'wide', 0, 0)]
  transfers between devices with their start and end apart: 32 -> 3, of which waited for: 24 -> 3; matrix products, arithmetic and copies ran while one was open for 0% -> 12% of each run, Pallas kernels for 0% -> 11%
where the time goes in v3:
time: 106 us; the launch traced here: 105 us
  Pallas kernels  34.6 us (33%)
  blocking collectives  27.2 us (26%)
  waiting for transfers between devices  14 us (13%)
  matrix products  12.1 us (11%)
  starting transfers between devices  11.5 us (11%)
  other arithmetic  2.45 us (2%)
  local copies, waits for them, and re-layouts  1.57 us (1%)
  between operations  1.34 us (1%)
    all_to_all x1, blocking collectives, reduced_rows(): own = jnp.sum(lax.all_to_all(share, AXES, 0, 0), axis=0)  14.2 us
    all_to_all x1, blocking collectives, reduced_rows(): return lax.all_to_all(copies, AXES, 0, 0).reshape(partial.shape)  13 us
    dot_general x1, matrix products, shards_whole(): jnp.einsum('bc,dc->bd', vflat, vflat, precision=lax.Precision.HIGHEST)  12.1 us
    pallas_call x1, Pallas kernels, basis_terms(): pl.pallas_call(functools.partial(basis_body, group=group, held=held), gri...  11.3 us
    pallas_call x1, Pallas kernels, solve_whole(): pl.pallas_call(functools.partial(solve_body, dims=(wide, narrow, near, ro...  10.6 us
    all_to_all x1, starting transfers between devices, solve_whole(): got = lax.all_to_all(sent, 'wide', 0, 0)  8.34 us
    all_to_all x1, waiting for transfers between devices, solve_whole(): lax.all_to_all(x.reshape(wide * narrow, chunk, rows, LANE), AXES, 0, 0)  8.28 us
    pallas_call x1, Pallas kernels, first_sums(): pl.pallas_call(functools.partial(first_body, dims=dims, count=count), gri...  5.51 us
  transfers between devices with their start and end apart: 3, of which 3 were waited for; matrix products, arithmetic and copies ran while one was open for 12% of the time, Pallas kernels for 11%

profile of v3, /device:TPU:0, one launch (start us, length us, event | category | flops | bytes accessed | tf_op | source)
XLA Modules:
  0.0 104.7 jit_solution(16967320836047039812)
XLA Ops:
  0.6 0.7 stack_broadcast_in_dim.2
  1.4 1.8 %pad_maximum_fusion = f32[16,2,4,8,128]{4,3,2,1,0:T(8,128)} fusion(f32[16,1,4,8,128]{4,3,2,1,0:T(8,128)S(1)} %stack_broadcast_in_dim.2, f32[16,1,4,8,128]{4,3,2,1,0:T(8,128)} %bitcast.23), kind=kLoop, calls=%fused_computation.5 | loop fusion | flops 131072 | bytes 1048576 | tf_op jit(solution)/shard_map/stack | solution.py:268
  3.2 8.3 %all-to-all-start.1 = ((f32[16,2,4,8,128]{4,3,2,1,0:T(8,128)}), f32[16,2,4,8,128]{4,3,2,1,0:T(8,128)S(1)}, u32[]{:S(2)}, u32[]{:S(2)}) async-start(f32[16,2,4,8,128]{4,3,2,1,0:T(8,128)} %pad_maximum_fusion), calls=%async_computation.1 | async-start | bytes 1048576 | tf_op jit(solution)/shard_map/all_to_all | solution.py:269
  11.5 11.3 %basis_terms.1 = (bf16[256,4096]{1,0:T(8,128)(2,1)S(1)}, bf16[256,4096]{1,0:T(8,128)(2,1)}, bf16[256,4096]{1,0:T(8,128)(2,1)}) custom-call(f32[8192,128]{1,0:T(8,128)} %bitcast.15), custom_call_target="tpu_custom_call" | custom-call | tf_op jit(solution)/shard_map/basis_terms/pallas_call | solution.py:312
  22.8 3.8 %all-to-all-done.1.refs_0_ = f32[16,2,4,8,128]{4,3,2,1,0:T(8,128)S(1)} async-done(((f32[16,2,4,8,128]{4,3,2,1,0:T(8,128)}), f32[16,2,4,8,128]{4,3,2,1,0:T(8,128)S(1)}, u32[]{:S(2)}, u32[]{:S(2)}) %all-to-all-start.1) | async-done | bytes 524320 | tf_op jit(solution)/shard_map/all_to_all | solution.py:269
  26.6 0.0 copy-start
  26.6 0.0 collective-permute-start
  26.6 1.9 %collective-permute-done.refs_1_ = f32[16,2,4,8,128]{4,3,2,1,0:T(8,128)S(1)} collective-permute-done((f32[16,2,4,8,128]{4,3,2,1,0:T(8,128)S(1)}, f32[16,2,4,8,128]{4,3,2,1,0:T(8,128)S(1)}, u32[]{:S(2)}, u32[]{:S(2)}) %collective-permute-start) | collective-permute-done | bytes 524320 | tf_op jit(solution)/shard_map/ppermute | solution.py:273
  28.5 0.0 copy-start.1
  28.5 0.0 copy-done
  28.5 0.8 copy-done.1
  29.3 10.6 %solve_whole.1 = f32[192,8,128]{2,1,0:T(8,128)} custom-call(s32[1]{0:T(128)} %bitcast.1.core_ref, f32[3]{0:T(128)} %shift_ref.1, f32[16,2,4,8,128]{4,3,2,1,0:T(8,128)} %copy-done, f32[16,2,4,8,128]{4,3,2,1,0:T(8,128)} %copy-done.1), custom_call_target="tpu_custom_call" | custom-call | tf_op jit(solution)/shard_map/solve_whole/pallas_call | solution.py:280
  40.0 3.1 %all-to-all-start.2 = ((f32[32,6,8,128]{3,2,1,0:T(8,128)}), f32[32,6,8,128]{3,2,1,0:T(8,128)S(1)}, u32[]{:S(2)}, u32[]{:S(2)}) async-start(f32[32,6,8,128]{3,2,1,0:T(8,128)} %bitcast.19), calls=%async_computation.2 | async-start | bytes 1572864 | tf_op jit(solution)/shard_map/all_to_all | solution.py:288
  43.1 12.1 %fusion.2.gram = f32[256,256]{1,0:T(8,128)} fusion(f32[256,4,8,128]{3,2,1,0:T(8,128)} %param.7), kind=kOutput, calls=%fused_computation.4 | convolution fusion | flops 3221225472 | bytes 4456448 | tf_op jit(solution)/shard_map/bc,dc->bd/dot_general | solution.py:524
  55.2 8.3 %all-to-all-done.2 = f32[32,6,8,128]{3,2,1,0:T(8,128)S(1)} async-done(((f32[32,6,8,128]{3,2,1,0:T(8,128)}), f32[32,6,8,128]{3,2,1,0:T(8,128)S(1)}, u32[]{:S(2)}, u32[]{:S(2)}) %all-to-all-start.2) | async-done | bytes 786464 | tf_op jit(solution)/shard_map/all_to_all | solution.py:288
  63.5 5.5 %first_sums.1 = f32[512,128]{1,0:T(8,128)} custom-call(f32[1536,128]{1,0:T(8,128)S(1)} %bitcast.16, f32[256,256]{1,0:T(8,128)} %fusion.2.gram, bf16[256,4096]{1,0:T(8,128)(2,1)S(1)} %get-tuple-element.40.high, bf16[256,4096]{1,0:T(8,128)(2,1)} %get-tuple-element.41.mid, bf16[256,4096]{1,0:T(8,128)(2,1)} %get-tuple-element.42.low), custom_call_target="tpu_custom_call" | custom-call | tf_op jit(solution)/shard_map/first_sums/pallas_call | solution.py:402
  69.0 14.2 %all_to_all.26 = f32[32,16,128]{2,1,0:T(8,128)S(1)} all-to-all(f32[32,16,128]{2,1,0:T(8,128)} %bitcast.21), channel_id=1, replica_groups=mesh['wide'=16,'narrow'=2] {'wide','narrow'}, dimensions={0} | all-to-all | bytes 524288 | tf_op jit(solution)/shard_map/all_to_all | solution.py:30
  83.3 13.0 %all_to_all.27 = f32[32,16,128]{2,1,0:T(8,128)} all-to-all(f32[32,16,128]{2,1,0:T(8,128)S(1)} %broadcast_in_dim.6), channel_id=1, replica_groups=mesh['wide'=16,'narrow'=2] {'wide','narrow'}, dimensions={0} | all-to-all | bytes 524288 | tf_op jit(solution)/shard_map/all_to_all | solution.py:32
  96.2 2.4 %coefficients_of.1 = (f32[48,256]{1,0:T(8,128)}, bf16[144,256]{1,0:T(8,128)(2,1)S(1)}, f32[48,128]{1,0:T(8,128)S(1)}, f32[1]{0:T(128)}) custom-call(f32[512,128]{1,0:T(8,128)} %bitcast.20), custom_call_target="tpu_custom_call" | custom-call | tf_op jit(solution)/shard_map/coefficients_of/pallas_call | solution.py:462
  99.3 4.8 %cleaned.3 = f32[48,32,128]{2,1,0:T(8,128)} custom-call(f32[1536,128]{1,0:T(8,128)S(1)} %bitcast.18, bf16[144,256]{1,0:T(8,128)(2,1)S(1)} %get-tuple-element.43.coef, f32[48,128]{1,0:T(8,128)S(1)} %get-tuple-element.47.mean_ref, bf16[256,4096]{1,0:T(8,128)(2,1)S(1)} %get-tuple-element.40.high, bf16[256,4096]{1,0:T(8,128)(2,1)} %get-tuple-element.41.mid, ...), custom_call_target="tpu_custom_call" | custom-call | tf_op jit(solution)/shard_map/cleaned/pallas_call | solution.py:508
  104.1 0.6 fusion.6
  (3 shorter events, 0.1 us)
Async XLA Ops:
  3.2 23.4 %all-to-all-start.1 = ((f32[16,2,4,8,128]{4,3,2,1,0:T(8,128)}), f32[16,2,4,8,128]{4,3,2,1,0:T(8,128)S(1)}, u32[]{:S(2)}, u32[]{:S(2)}) async-start(f32[16,2,4,8,128]{4,3,2,1,0:T(8,128)} %pad_maximum_fusion), calls=%async_computation.1 | async-start | bytes 1048576 | tf_op jit(solution)/shard_map/all_to_all | solution.py:269
  26.6 1.9 %copy-start = (f32[16,2,4,8,128]{4,3,2,1,0:T(8,128)}, f32[16,2,4,8,128]{4,3,2,1,0:T(8,128)S(1)}, u32[]{:S(2)}) copy-start(f32[16,2,4,8,128]{4,3,2,1,0:T(8,128)S(1)} %all-to-all-done.1.refs_0_) | copy-start | bytes 1572868
  26.6 1.9 %collective-permute-start = (f32[16,2,4,8,128]{4,3,2,1,0:T(8,128)S(1)}, f32[16,2,4,8,128]{4,3,2,1,0:T(8,128)S(1)}, u32[]{:S(2)}, u32[]{:S(2)}) collective-permute-start(f32[16,2,4,8,128]{4,3,2,1,0:T(8,128)S(1)} %all-to-all-done.1.refs_0_), channel_id=1, source_target_pairs={{1,0},{0,1},{3,2},{2,3},{5,4},{4,5},{7,6},{6,7},{9,8},{8,9},{11,10... | collective-permute-start | bytes 1572872 | tf_op jit(solution)/shard_map/ppermute | solution.py:273
  28.5 0.8 copy-start.1
  40.0 23.5 %all-to-all-start.2 = ((f32[32,6,8,128]{3,2,1,0:T(8,128)}), f32[32,6,8,128]{3,2,1,0:T(8,128)S(1)}, u32[]{:S(2)}, u32[]{:S(2)}) async-start(f32[32,6,8,128]{3,2,1,0:T(8,128)} %bitcast.19), calls=%async_computation.2 | async-start | bytes 1572864 | tf_op jit(solution)/shard_map/all_to_all | solution.py:288

commit v4 on v3

--- a/solution.py
+++ b/solution.py
@@ -12,6 +12,7 @@
 AXES = ("wide", "narrow")
 SUB, LANE = 8, 128
 UNROLL = 64
+MIB = 2**20
 
 
 def spread(coef):
@@ -106,8 +107,8 @@
     slots = own + left
     planes, height = wide * near, narrow * rows
     parts, out_ref, (shadow, cond), per = refs[:narrow], refs[narrow], refs[narrow + 1 : narrow + 3], refs[narrow + 3 :]
-    names = ("x", "r", "v", "t", "p", "s")
-    col = [dict(zip(names, per[6 * a : 6 * a + 6])) for a in range(slots)]
+    names = ("x", "r", "v", "t", "diag", "p", "s")
+    col = [dict(zip(names, per[7 * a : 7 * a + 7])) for a in range(slots)]
     core = core_ref[0]
     zero = jnp.zeros((SUB, LANE), jnp.float32)
     lane = lax.broadcasted_iota(jnp.int32, (SUB, LANE), 1)
@@ -139,13 +140,13 @@
     def inner(ref, i, y):
         return ref[i + 1, SUB + y : 2 * SUB + y, :]
 
-    def image(ref, i, y, here, c, shift):
+    def image(ref, i, y, here, c, diag):
         nb = ref[i, SUB + y : 2 * SUB + y, :] + ref[i + 2, SUB + y : 2 * SUB + y, :]
         nb = nb + (ref[i + 1, SUB + y - 1 : 2 * SUB + y - 1, :] + ref[i + 1, SUB + y + 1 : 2 * SUB + y + 1, :])
         nb = nb + (
             jnp.where(first_lane, 0.0, pltpu.roll(here, 1, 1)) + jnp.where(last_lane, 0.0, pltpu.roll(here, LANE - 1, 1))
         )
-        return c * (6.0 * here - nb) + shift * here
+        return at_tile(diag, i, y) * here - c * nb
 
     def mean(acc):
         total = jnp.sum(jnp.sum(acc, axis=1, keepdims=True), axis=0, keepdims=True) / total_cells
@@ -168,10 +169,12 @@
 
     def start(i, y, acc):
         b = at_tile(shadow, i, y)
+        six = 6.0 * at_tile(cond, i, y)
         for a in range(slots):
             col[a]["p"][i + 1, SUB + y : 2 * SUB + y, :] = b
             col[a]["r"][i, y : y + SUB, :] = b
             col[a]["x"][i, y : y + SUB, :] = zero
+            col[a]["diag"][i, y : y + SUB, :] = six + shift[a]
         return acc + b * b
 
     def half_step(rho, last):
@@ -180,7 +183,7 @@
             out = []
             for a in range(slots):
                 p = col[a]["p"]
-                v = image(p, i, y, inner(p, i, y), c, shift[a])
+                v = image(p, i, y, inner(p, i, y), c, col[a]["diag"])
                 col[a]["v"][i, y : y + SUB, :] = v
                 out.append(acc[a] + b * v)
             return tuple(out)
@@ -202,7 +205,7 @@
             for a in range(slots):
                 ref = col[a]["s"]
                 s = inner(ref, i, y)
-                t = image(ref, i, y, s, c, shift[a])
+                t = image(ref, i, y, s, c, col[a]["diag"])
                 one = [acc[a][0] + t * s, acc[a][1] + t * t]
                 if not last:
                     col[a]["t"][i, y : y + SUB, :] = t
@@ -259,14 +262,37 @@
     lax.fori_loop(0, wide, send, 0)
 
 
+def pack_body(inputs, conductance, out_ref, sems):
+    wide = inputs.shape[0]
+    copies = [pltpu.make_async_copy(inputs, out_ref.at[:, 0], sems.at[0])]
+    for w in range(wide):
+        copies.append(pltpu.make_async_copy(conductance, out_ref.at[w, 1], sems.at[w + 1]))
+    for copy in copies:
+        copy.start()
+    for copy in copies:
+        copy.wait()
+
+
+def packed(inputs, conductance):
+    anywhere = pl.BlockSpec(memory_space=pltpu.HBM)
+    return pl.pallas_call(
+        pack_body,
+        out_shape=jax.ShapeDtypeStruct((inputs.shape[0], 2) + inputs.shape[1:], jnp.float32),
+        in_specs=[anywhere, anywhere],
+        out_specs=anywhere,
+        scratch_shapes=[pltpu.SemaphoreType.DMA((inputs.shape[0] + 1,))],
+        compiler_params=pltpu.CompilerParams(vmem_limit_bytes=8 * MIB),
+        name="packed",
+    )(inputs, conductance)
+
+
 def solve_whole(inputs, conductance, shifts, total_cells, beside):
     wide, narrow = lax.axis_size("wide"), lax.axis_size("narrow")
     columns, near, rows, lanes = inputs.shape
     count = shifts.shape[0]
     own, left = split_columns(count, narrow)
     slots = own + left
-    sent = jnp.stack([inputs, jnp.broadcast_to(conductance[None], inputs.shape)], axis=1)
-    got = lax.all_to_all(sent, "wide", 0, 0)
+    got = lax.all_to_all(packed(inputs, conductance), "wide", 0, 0)
     got, beside = lax.optimization_barrier((got, beside))
     parts = [got]
     for step in range(1, narrow):
@@ -282,7 +308,8 @@
         out_shape=jax.ShapeDtypeStruct((wide * narrow * chunk, rows, LANE), jnp.float32),
         in_specs=[smem, smem] + [vmem] * narrow,
         out_specs=vmem,
-        scratch_shapes=[plain, plain] + [plain, plain, plain, plain, ringed, ringed] * slots,
+        scratch_shapes=[plain, plain] + [plain, plain, plain, plain, plain, ringed, ringed] * slots,
+        compiler_params=pltpu.CompilerParams(vmem_limit_bytes=24 * MIB),
         name="solve_whole",
     )(lax.axis_index("narrow").reshape(1), shifts, *parts)
     return lax.all_to_all(x.reshape(wide * narrow, chunk, rows, LANE), AXES, 0, 0), beside
@@ -315,8 +342,35 @@
         out_shape=(out,) * 3,
         in_specs=[pl.BlockSpec((group * held, LANE), lambda g: (g, 0))],
         out_specs=(pl.BlockSpec((group, held * LANE), lambda g: (g, 0)),) * 3,
+        compiler_params=pltpu.CompilerParams(vmem_limit_bytes=8 * MIB),
         name="basis_terms",
     )(old_basis.reshape(-1, LANE))
+
+
+def gram_body(high, mid, low, out_ref):
+    def against(left, right):
+        return lax.dot_general(
+            left[...], right[...], (((1,), (1,)), ((), ())), preferred_element_type=jnp.float32
+        )
+
+    across = against(high, mid) + against(high, low)
+    out_ref[...] = against(high, high) + (against(mid, mid) + (across + across.T))
+
+
+def gram_of_terms(parts):
+    basis = parts[0].shape[0]
+    vmem = pl.BlockSpec(memory_space=pltpu.VMEM)
+    return pl.pallas_call(
+        gram_body,
+        out_shape=jax.ShapeDtypeStruct((basis, basis), jnp.float32),
+        in_specs=[vmem] * 3,
+        out_specs=vmem,
+        cost_estimate=pl.CostEstimate(
+            flops=8 * basis * parts[0].size, bytes_accessed=6 * parts[0].size, transcendentals=0
+        ),
+        compiler_params=pltpu.CompilerParams(vmem_limit_bytes=16 * MIB),
+        name="gram_of_terms",
+    )(*parts)
 
 
 def column_row(j, xl, y, dims, count):
@@ -410,6 +464,7 @@
             pltpu.VMEM((width, basis), jnp.float32),
             pltpu.VMEM((LANE, LANE), jnp.float32),
         ],
+        compiler_params=pltpu.CompilerParams(vmem_limit_bytes=16 * MIB),
         name="first_sums",
     )(x, gram, *parts)
 
@@ -469,15 +524,23 @@
         ),
         in_specs=[vmem],
         out_specs=(vmem, vmem, vmem, pl.BlockSpec(memory_space=pltpu.SMEM)),
+        compiler_params=pltpu.CompilerParams(vmem_limit_bytes=8 * MIB),
         name="coefficients_of",
     )(sums)
 
 
-def clean_body(x_ref, coef, mean_ref, high, mid, low, out_ref, *, dims, count, scaled):
+def clean_body(x_ref, coef, mean_ref, high, mid, low, out_ref, scale_ref, *, dims, count, scaled):
     wide, narrow, near, rows = dims
     width = wide * count
     xl = pl.program_id(0)
     flat = out_ref.reshape(width * rows, LANE)
+
+    @pl.when(xl == 0)
+    def _():
+        shape = (width, LANE)
+        same = lax.broadcasted_iota(jnp.int32, shape, 0) == lax.broadcasted_iota(jnp.int32, shape, 1)
+        scale = jnp.sqrt(mean_ref[...] + 1e-06)
+        scale_ref[...] = jnp.sum(jnp.where(same, scale, 0.0), axis=0, keepdims=True)[:, :width]
 
     def against(rows_used, part):
         return lax.dot_general(
@@ -508,9 +571,13 @@
     return pl.pallas_call(
         functools.partial(clean_body, dims=dims, count=count, scaled=scaled),
         grid=(near,),
-        out_shape=jax.ShapeDtypeStruct((width, near * rows, LANE), jnp.float32),
+        out_shape=(
+            jax.ShapeDtypeStruct((width, near * rows, LANE), jnp.float32),
+            jax.ShapeDtypeStruct((1, width), jnp.float32),
+        ),
         in_specs=[vmem, vmem, vmem, cells, cells, cells],
-        out_specs=pl.BlockSpec((width, rows, LANE), lambda g: (0, g, 0)),
+        out_specs=(pl.BlockSpec((width, rows, LANE), lambda g: (0, g, 0)), pl.BlockSpec((1, width), lambda g: (0, 0))),
+        compiler_params=pltpu.CompilerParams(vmem_limit_bytes=16 * MIB),
         name="cleaned",
     )(x, coef_terms, mean_square, *parts)
 
@@ -520,23 +587,21 @@
     columns, near, rows, _ = inputs.shape
     count, basis = shifts.shape[0], old_basis.shape[0]
     width, dims = columns * count, (wide, narrow, near, rows)
-    vflat = old_basis.reshape(basis, -1)
-    gram = jnp.einsum("bc,dc->bd", vflat, vflat, precision=lax.Precision.HIGHEST)
     parts = basis_terms(old_basis)
     x, parts = solve_whole(inputs, conductance, shifts, total_cells, parts)
     x = x.reshape(-1, LANE)
+    gram = gram_of_terms(parts)
     sums = reduced_rows(first_sums(x, gram, parts, dims, count))
     coef, coef_terms, quick, bad = coefficients_of(sums, width, basis, total_cells)
 
     def slow():
-        twice = cleaned(x, coef_terms, quick, parts, dims, count, False)
+        twice, _ = cleaned(x, coef_terms, quick, parts, dims, count, False)
         total = reduced(jnp.sum(twice * twice, axis=(1, 2))) / total_cells
         return jnp.broadcast_to(total[:, None], quick.shape)
 
     mean_square = lax.cond(bad[0] == 0.0, lambda: quick, slow)
-    new_columns = cleaned(x, coef_terms, mean_square, parts, dims, count, True)
-    col_scale = jnp.sqrt(mean_square[:, 0] + 1e-06)
-    return (new_columns.reshape((width,) + inputs.shape[1:]), coef.T, col_scale)
+    new_columns, col_scale = cleaned(x, coef_terms, mean_square, parts, dims, count, True)
+    return (new_columns.reshape((width,) + inputs.shape[1:]), coef.T, col_scale.reshape(-1))
 
 
 def shards_spread(inputs, old_basis, conductance, shifts, total_cells):
@@ -567,7 +632,7 @@
         and wide * near % UNROLL == 0
         and old_basis.shape[0] % LANE == 0
         and columns * shifts.shape[0] <= LANE
-        and field * (6 + 8 * (own + left)) <= 24 * 2**20
+        and field * (6 + 10 * (own + left)) <= 24 * 2**20
         and old_basis.size * 4 <= 8 * 2**20
     )
 

time: 106 us -> 101 us (0.953)
  matrix products: 12.1 us -> 0 us
  waiting for transfers between devices: 14 us -> 23.4 us
  other arithmetic: 2.45 us -> 0.04 us
  local copies, waits for them, and re-layouts: 1.57 us -> 3.87 us
    dot_general x1 -> x0, matrix products: 12.1 us -> none  [shards_whole(): jnp.einsum('bc,dc->bd', vflat, vflat, precision=lax.Precision.HIGHEST)]
    all_to_all x1, waiting for transfers between devices: 8.28 us -> 15.9 us  [solve_whole(): lax.all_to_all(x.reshape(wide * narrow, chunk, rows, LANE), AXES, 0, 0)]
    pallas_call x0 -> x2, Pallas kernels: none -> 5.56 us  [the longest x1 4.64 us: gram_of_terms(): pl.pallas_call(gram_body, out_shape=jax.ShapeDtypeStruct((basis, basis),...]
    pallas_call x1, Pallas kernels: 11.3 us -> 7.34 us  [basis_terms(): pl.pallas_call(functools.partial(basis_body, group=group, held=held), gri...]
    unnamed x4 -> x8, local copies, waits for them, and re-layouts: 0.82 us -> 3.85 us
    another operation x1 -> x0, other arithmetic: 1.79 us -> none  [solve_whole(): jnp.stack([inputs, jnp.broadcast_to(conductance[None], inputs.shape)], ax...]
    all_to_all x1, waiting for transfers between devices: 3.78 us -> 5.55 us  [solve_whole(): got = lax.all_to_all(packed(inputs, conductance), 'wide', 0, 0)]
  transfers between devices with their start and end apart: 3 -> 3, of which waited for: 3 -> 3; matrix products, arithmetic and copies ran while one was open for 12% -> 0% of each run, Pallas kernels for 11% -> 12%
where the time goes in v4:
time: 101 us; the launch traced here: 100 us
  Pallas kernels  33.7 us (33%)
  blocking collectives  26.8 us (27%)
  waiting for transfers between devices  23.4 us (23%)
  starting transfers between devices  11.3 us (11%)
  local copies, waits for them, and re-layouts  3.87 us (4%)
  between operations  1.36 us (1%)
    all_to_all x1, waiting for transfers between devices, solve_whole(): lax.all_to_all(x.reshape(wide * narrow, chunk, rows, LANE), AXES, 0, 0)  15.9 us
    all_to_all x1, blocking collectives, reduced_rows(): own = jnp.sum(lax.all_to_all(share, AXES, 0, 0), axis=0)  14 us
    all_to_all x1, blocking collectives, reduced_rows(): return lax.all_to_all(copies, AXES, 0, 0).reshape(partial.shape)  12.8 us
    pallas_call x1, Pallas kernels, solve_whole(): pl.pallas_call(functools.partial(solve_body, dims=(wide, narrow, near, ro...  9.87 us
    all_to_all x1, starting transfers between devices, solve_whole(): got = lax.all_to_all(packed(inputs, conductance), 'wide', 0, 0)  8.35 us
    pallas_call x1, Pallas kernels, basis_terms(): pl.pallas_call(functools.partial(basis_body, group=group, held=held), gri...  7.34 us
    all_to_all x1, waiting for transfers between devices, solve_whole(): got = lax.all_to_all(packed(inputs, conductance), 'wide', 0, 0)  5.55 us
    pallas_call x1, Pallas kernels, cleaned(): pl.pallas_call(functools.partial(clean_body, dims=dims, count=count, scal...  4.79 us
  transfers between devices with their start and end apart: 3, of which 3 were waited for; matrix products, arithmetic and copies ran while one was open for 0% of the time, Pallas kernels for 12%

profile of v4, /device:TPU:0, one launch (start us, length us, event | category | flops | bytes accessed | tf_op | source)
XLA Modules:
  0.0 100.4 jit_solution(12982457780899486080)
XLA Ops:
  0.6 0.0 copy-start.1
  0.6 0.9 copy-done.1
  1.6 0.0 copy-start.2
  1.6 0.7 copy-done.2
  2.3 0.9 packed.1
  3.2 8.4 %all-to-all-start.1 = ((f32[16,2,4,8,128]{4,3,2,1,0:T(8,128)}), f32[16,2,4,8,128]{4,3,2,1,0:T(8,128)S(1)}, u32[]{:S(2)}, u32[]{:S(2)}) async-start(f32[16,2,4,8,128]{4,3,2,1,0:T(8,128)} %packed.1), calls=%async_computation.1 | async-start | bytes 1048576 | tf_op jit(solution)/shard_map/all_to_all | solution.py:295
  11.6 0.0 copy-start
  11.6 2.2 %copy-done = f32[256,4,8,128]{3,2,1,0:T(8,128)S(1)} copy-done((f32[256,4,8,128]{3,2,1,0:T(8,128)S(1)}, f32[256,4,8,128]{3,2,1,0:T(8,128)}, u32[]{:S(2)}) %copy-start) | copy-done | bytes 4194328
  13.8 0.0 copy-start.3
  13.8 7.3 %basis_terms.1 = (bf16[256,4096]{1,0:T(8,128)(2,1)S(1)}, bf16[256,4096]{1,0:T(8,128)(2,1)}, bf16[256,4096]{1,0:T(8,128)(2,1)}) custom-call(f32[8192,128]{1,0:T(8,128)S(1)} %bitcast.11), custom_call_target="tpu_custom_call" | custom-call | tf_op jit(solution)/shard_map/basis_terms/pallas_call | solution.py:339
  21.1 5.5 %all-to-all-done.1.refs_0_ = f32[16,2,4,8,128]{4,3,2,1,0:T(8,128)S(1)} async-done(((f32[16,2,4,8,128]{4,3,2,1,0:T(8,128)}), f32[16,2,4,8,128]{4,3,2,1,0:T(8,128)S(1)}, u32[]{:S(2)}, u32[]{:S(2)}) %all-to-all-start.1) | async-done | bytes 524320 | tf_op jit(solution)/shard_map/all_to_all | solution.py:295
  26.7 0.0 collective-permute-start
  26.7 1.9 %collective-permute-done.refs_1_ = f32[16,2,4,8,128]{4,3,2,1,0:T(8,128)S(1)} collective-permute-done((f32[16,2,4,8,128]{4,3,2,1,0:T(8,128)S(1)}, f32[16,2,4,8,128]{4,3,2,1,0:T(8,128)S(1)}, u32[]{:S(2)}, u32[]{:S(2)}) %collective-permute-start) | collective-permute-done | bytes 524320 | tf_op jit(solution)/shard_map/ppermute | solution.py:299
  28.6 0.0 copy-done.3
  28.6 9.9 %solve_whole.1 = f32[192,8,128]{2,1,0:T(8,128)} custom-call(s32[1]{0:T(128)} %bitcast.1.core_ref, f32[3]{0:T(128)S(1)} %copy-done.3, f32[16,2,4,8,128]{4,3,2,1,0:T(8,128)S(1)} %all-to-all-done.1.refs_0_, f32[16,2,4,8,128]{4,3,2,1,0:T(8,128)S(1)} %collective-permute-done.refs_1_), custom_call_target="tpu_custom_call" | custom-call | tf_op jit(solution)/shard_map/solve_whole/pallas_call | solution.py:306
  38.5 2.9 %all-to-all-start.2 = ((f32[32,6,8,128]{3,2,1,0:T(8,128)}), f32[32,6,8,128]{3,2,1,0:T(8,128)S(1)}, u32[]{:S(2)}, u32[]{:S(2)}) async-start(f32[32,6,8,128]{3,2,1,0:T(8,128)} %bitcast.3), calls=%async_computation.2 | async-start | bytes 1572864 | tf_op jit(solution)/shard_map/all_to_all | solution.py:315
  41.4 4.6 %gram_of_terms.1.gram = f32[256,256]{1,0:T(8,128)S(1)} custom-call(bf16[256,4096]{1,0:T(8,128)(2,1)S(1)} %get-tuple-element.43.high, bf16[256,4096]{1,0:T(8,128)(2,1)} %get-tuple-element.44.mid, bf16[256,4096]{1,0:T(8,128)(2,1)} %get-tuple-element.45.low), custom_call_target="tpu_custom_call" | custom-call | flops 2147483648 | bytes 6291456 | tf_op jit(solution)/shard_map/gram_of_terms/pallas_call | solution.py:363
  46.0 15.9 %all-to-all-done.2 = f32[32,6,8,128]{3,2,1,0:T(8,128)S(1)} async-done(((f32[32,6,8,128]{3,2,1,0:T(8,128)}), f32[32,6,8,128]{3,2,1,0:T(8,128)S(1)}, u32[]{:S(2)}, u32[]{:S(2)}) %all-to-all-start.2) | async-done | bytes 786464 | tf_op jit(solution)/shard_map/all_to_all | solution.py:315
  62.0 4.7 %first_sums.1 = f32[512,128]{1,0:T(8,128)S(1)} custom-call(f32[1536,128]{1,0:T(8,128)S(1)} %bitcast.14, f32[256,256]{1,0:T(8,128)S(1)} %gram_of_terms.1.gram, bf16[256,4096]{1,0:T(8,128)(2,1)S(1)} %get-tuple-element.43.high, bf16[256,4096]{1,0:T(8,128)(2,1)} %get-tuple-element.44.mid, bf16[256,4096]{1,0:T(8,128)(2,1)} %get-tuple-element.45.low), custom_call_target="tpu_custom_call" | custom-call | tf_op jit(solution)/shard_map/first_sums/pallas_call | solution.py:456
  66.7 14.0 %all_to_all.26 = f32[32,16,128]{2,1,0:T(8,128)S(1)} all-to-all(f32[32,16,128]{2,1,0:T(8,128)S(1)} %bitcast.13), channel_id=1, replica_groups=mesh['wide'=16,'narrow'=2] {'wide','narrow'}, dimensions={0} | all-to-all | bytes 524288 | tf_op jit(solution)/shard_map/all_to_all | solution.py:31
  80.8 12.8 %all_to_all.27 = f32[32,16,128]{2,1,0:T(8,128)S(1)} all-to-all(f32[32,16,128]{2,1,0:T(8,128)S(1)} %broadcast_in_dim.6), channel_id=1, replica_groups=mesh['wide'=16,'narrow'=2] {'wide','narrow'}, dimensions={0} | all-to-all | bytes 524288 | tf_op jit(solution)/shard_map/all_to_all | solution.py:33
  93.5 1.4 %coefficients_of.1 = (f32[48,256]{1,0:T(8,128)}, bf16[144,256]{1,0:T(8,128)(2,1)S(1)}, f32[48,128]{1,0:T(8,128)S(1)}, f32[1]{0:T(128)}) custom-call(f32[512,128]{1,0:T(8,128)S(1)} %bitcast.12), custom_call_target="tpu_custom_call" | custom-call | tf_op jit(solution)/shard_map/coefficients_of/pallas_call | solution.py:517
  95.7 4.8 %cleaned.3 = (f32[48,32,128]{2,1,0:T(8,128)}, f32[1,48]{1,0:T(1,128)}) custom-call(f32[1536,128]{1,0:T(8,128)S(1)} %bitcast.16, bf16[144,256]{1,0:T(8,128)(2,1)S(1)} %get-tuple-element.46.coef, f32[48,128]{1,0:T(8,128)S(1)} %get-tuple-element.52.mean_ref, bf16[256,4096]{1,0:T(8,128)(2,1)S(1)} %get-tuple-element.43.high, ...), custom_call_target="tpu_custom_call" | custom-call | tf_op jit(solution)/shard_map/cleaned/pallas_call | solution.py:571
  (3 shorter events, 0.1 us)
Async XLA Ops:
  0.6 1.0 copy-start.1
  1.6 0.7 copy-start.2
  3.2 23.4 %all-to-all-start.1 = ((f32[16,2,4,8,128]{4,3,2,1,0:T(8,128)}), f32[16,2,4,8,128]{4,3,2,1,0:T(8,128)S(1)}, u32[]{:S(2)}, u32[]{:S(2)}) async-start(f32[16,2,4,8,128]{4,3,2,1,0:T(8,128)} %packed.1), calls=%async_computation.1 | async-start | bytes 1048576 | tf_op jit(solution)/shard_map/all_to_all | solution.py:295
  11.6 2.2 %copy-start = (f32[256,4,8,128]{3,2,1,0:T(8,128)S(1)}, f32[256,4,8,128]{3,2,1,0:T(8,128)}, u32[]{:S(2)}) copy-start(f32[256,4,8,128]{3,2,1,0:T(8,128)} %param.7) | copy-start | bytes 12582916
  13.8 14.8 %copy-start.3 = (f32[3]{0:T(128)S(1)}, f32[3]{0:T(128)}, u32[]{:S(2)}) copy-start(f32[3]{0:T(128)} %shift_ref.1) | copy-start | bytes 40
  26.7 1.9 %collective-permute-start = (f32[16,2,4,8,128]{4,3,2,1,0:T(8,128)S(1)}, f32[16,2,4,8,128]{4,3,2,1,0:T(8,128)S(1)}, u32[]{:S(2)}, u32[]{:S(2)}) collective-permute-start(f32[16,2,4,8,128]{4,3,2,1,0:T(8,128)S(1)} %all-to-all-done.1.refs_0_), channel_id=1, source_target_pairs={{1,0},{0,1},{3,2},{2,3},{5,4},{4,5},{7,6},{6,7},{9,8},{8,9},{11,10... | collective-permute-start | bytes 1572872 | tf_op jit(solution)/shard_map/ppermute | solution.py:299
  38.5 23.5 %all-to-all-start.2 = ((f32[32,6,8,128]{3,2,1,0:T(8,128)}), f32[32,6,8,128]{3,2,1,0:T(8,128)S(1)}, u32[]{:S(2)}, u32[]{:S(2)}) async-start(f32[32,6,8,128]{3,2,1,0:T(8,128)} %bitcast.3), calls=%async_computation.2 | async-start | bytes 1572864 | tf_op jit(solution)/shard_map/all_to_all | solution.py:315

commit v5 on v4

--- a/solution.py
+++ b/solution.py
@@ -262,26 +262,20 @@
     lax.fori_loop(0, wide, send, 0)
 
 
-def pack_body(inputs, conductance, out_ref, sems):
-    wide = inputs.shape[0]
-    copies = [pltpu.make_async_copy(inputs, out_ref.at[:, 0], sems.at[0])]
-    for w in range(wide):
-        copies.append(pltpu.make_async_copy(conductance, out_ref.at[w, 1], sems.at[w + 1]))
-    for copy in copies:
-        copy.start()
-    for copy in copies:
-        copy.wait()
+def pack_body(inputs, conductance, out_ref):
+    cond = conductance[...]
+    for w in range(inputs.shape[0]):
+        out_ref[w, 0] = inputs[w]
+        out_ref[w, 1] = cond
 
 
 def packed(inputs, conductance):
-    anywhere = pl.BlockSpec(memory_space=pltpu.HBM)
+    vmem = pl.BlockSpec(memory_space=pltpu.VMEM)
     return pl.pallas_call(
         pack_body,
         out_shape=jax.ShapeDtypeStruct((inputs.shape[0], 2) + inputs.shape[1:], jnp.float32),
-        in_specs=[anywhere, anywhere],
-        out_specs=anywhere,
-        scratch_shapes=[pltpu.SemaphoreType.DMA((inputs.shape[0] + 1,))],
-        compiler_params=pltpu.CompilerParams(vmem_limit_bytes=8 * MIB),
+        in_specs=[vmem, vmem],
+        out_specs=vmem,
         name="packed",
     )(inputs, conductance)
 

time: 101 us -> 100 us (0.990)
  local copies, waits for them, and re-layouts: 3.87 us -> 2.21 us
    unnamed x8 -> x4, local copies, waits for them, and re-layouts: 3.85 us -> 2.19 us
where the time goes in v5:
time: 100 us; the launch traced here: 99.6 us
  Pallas kernels  34.6 us (35%)
  blocking collectives  26.8 us (27%)
  waiting for transfers between devices  23.4 us (23%)
  starting transfers between devices  11.3 us (11%)
  local copies, waits for them, and re-layouts  2.21 us (2%)
  between operations  1.34 us (1%)
    all_to_all x1, waiting for transfers between devices, solve_whole(): lax.all_to_all(x.reshape(wide * narrow, chunk, rows, LANE), AXES, 0, 0)  15.9 us
    all_to_all x1, blocking collectives, reduced_rows(): own = jnp.sum(lax.all_to_all(share, AXES, 0, 0), axis=0)  14 us
    all_to_all x1, blocking collectives, reduced_rows(): return lax.all_to_all(copies, AXES, 0, 0).reshape(partial.shape)  12.8 us
    pallas_call x1, Pallas kernels, solve_whole(): pl.pallas_call(functools.partial(solve_body, dims=(wide, narrow, near, ro...  9.87 us
    all_to_all x1, starting transfers between devices, solve_whole(): got = lax.all_to_all(packed(inputs, conductance), 'wide', 0, 0)  8.34 us
    pallas_call x1, Pallas kernels, basis_terms(): pl.pallas_call(functools.partial(basis_body, group=group, held=held), gri...  7.35 us
    all_to_all x1, waiting for transfers between devices, solve_whole(): got = lax.all_to_all(packed(inputs, conductance), 'wide', 0, 0)  5.54 us
    pallas_call x1, Pallas kernels, cleaned(): pl.pallas_call(functools.partial(clean_body, dims=dims, count=count, scal...  4.79 us
  transfers between devices with their start and end apart: 3, of which 3 were waited for; matrix products, arithmetic and copies ran while one was open for 0% of the time, Pallas kernels for 12%

profile of v5, /device:TPU:0, one launch (start us, length us, event | category | flops | bytes accessed | tf_op | source)
XLA Modules:
  0.0 99.6 jit_solution(4748274822922815259)
XLA Ops:
  0.6 1.8 %packed.1 = f32[16,2,4,8,128]{4,3,2,1,0:T(8,128)} custom-call(f32[16,4,8,128]{3,2,1,0:T(8,128)} %inputs.1, f32[4,8,128]{2,1,0:T(8,128)} %conductance.1), custom_call_target="tpu_custom_call" | custom-call | tf_op jit(solution)/shard_map/packed/pallas_call | solution.py:274
  2.4 8.3 %all-to-all-start.1 = ((f32[16,2,4,8,128]{4,3,2,1,0:T(8,128)}), f32[16,2,4,8,128]{4,3,2,1,0:T(8,128)S(1)}, u32[]{:S(2)}, u32[]{:S(2)}) async-start(f32[16,2,4,8,128]{4,3,2,1,0:T(8,128)} %packed.1), calls=%async_computation.1 | async-start | bytes 1048576 | tf_op jit(solution)/shard_map/all_to_all | solution.py:289
  10.8 0.0 copy-start
  10.8 2.2 %copy-done = f32[256,4,8,128]{3,2,1,0:T(8,128)S(1)} copy-done((f32[256,4,8,128]{3,2,1,0:T(8,128)S(1)}, f32[256,4,8,128]{3,2,1,0:T(8,128)}, u32[]{:S(2)}) %copy-start) | copy-done | bytes 4194328
  13.0 0.0 copy-start.1
  13.0 7.3 %basis_terms.1 = (bf16[256,4096]{1,0:T(8,128)(2,1)S(1)}, bf16[256,4096]{1,0:T(8,128)(2,1)}, bf16[256,4096]{1,0:T(8,128)(2,1)}) custom-call(f32[8192,128]{1,0:T(8,128)S(1)} %bitcast.11), custom_call_target="tpu_custom_call" | custom-call | tf_op jit(solution)/shard_map/basis_terms/pallas_call | solution.py:333
  20.3 5.5 %all-to-all-done.1.refs_0_ = f32[16,2,4,8,128]{4,3,2,1,0:T(8,128)S(1)} async-done(((f32[16,2,4,8,128]{4,3,2,1,0:T(8,128)}), f32[16,2,4,8,128]{4,3,2,1,0:T(8,128)S(1)}, u32[]{:S(2)}, u32[]{:S(2)}) %all-to-all-start.1) | async-done | bytes 524320 | tf_op jit(solution)/shard_map/all_to_all | solution.py:289
  25.8 0.0 collective-permute-start
  25.9 1.9 %collective-permute-done.refs_1_ = f32[16,2,4,8,128]{4,3,2,1,0:T(8,128)S(1)} collective-permute-done((f32[16,2,4,8,128]{4,3,2,1,0:T(8,128)S(1)}, f32[16,2,4,8,128]{4,3,2,1,0:T(8,128)S(1)}, u32[]{:S(2)}, u32[]{:S(2)}) %collective-permute-start) | collective-permute-done | bytes 524320 | tf_op jit(solution)/shard_map/ppermute | solution.py:293
  27.8 0.0 copy-done.1
  27.8 9.9 %solve_whole.1 = f32[192,8,128]{2,1,0:T(8,128)} custom-call(s32[1]{0:T(128)} %bitcast.1.core_ref, f32[3]{0:T(128)S(1)} %copy-done.1, f32[16,2,4,8,128]{4,3,2,1,0:T(8,128)S(1)} %all-to-all-done.1.refs_0_, f32[16,2,4,8,128]{4,3,2,1,0:T(8,128)S(1)} %collective-permute-done.refs_1_), custom_call_target="tpu_custom_call" | custom-call | tf_op jit(solution)/shard_map/solve_whole/pallas_call | solution.py:300
  37.6 2.9 %all-to-all-start.2 = ((f32[32,6,8,128]{3,2,1,0:T(8,128)}), f32[32,6,8,128]{3,2,1,0:T(8,128)S(1)}, u32[]{:S(2)}, u32[]{:S(2)}) async-start(f32[32,6,8,128]{3,2,1,0:T(8,128)} %bitcast.3), calls=%async_computation.2 | async-start | bytes 1572864 | tf_op jit(solution)/shard_map/all_to_all | solution.py:309
  40.6 4.6 %gram_of_terms.1.gram = f32[256,256]{1,0:T(8,128)S(1)} custom-call(bf16[256,4096]{1,0:T(8,128)(2,1)S(1)} %get-tuple-element.43.high, bf16[256,4096]{1,0:T(8,128)(2,1)} %get-tuple-element.44.mid, bf16[256,4096]{1,0:T(8,128)(2,1)} %get-tuple-element.45.low), custom_call_target="tpu_custom_call" | custom-call | flops 2147483648 | bytes 6291456 | tf_op jit(solution)/shard_map/gram_of_terms/pallas_call | solution.py:357
  45.2 15.9 %all-to-all-done.2 = f32[32,6,8,128]{3,2,1,0:T(8,128)S(1)} async-done(((f32[32,6,8,128]{3,2,1,0:T(8,128)}), f32[32,6,8,128]{3,2,1,0:T(8,128)S(1)}, u32[]{:S(2)}, u32[]{:S(2)}) %all-to-all-start.2) | async-done | bytes 786464 | tf_op jit(solution)/shard_map/all_to_all | solution.py:309
  61.2 4.7 %first_sums.1 = f32[512,128]{1,0:T(8,128)S(1)} custom-call(f32[1536,128]{1,0:T(8,128)S(1)} %bitcast.14, f32[256,256]{1,0:T(8,128)S(1)} %gram_of_terms.1.gram, bf16[256,4096]{1,0:T(8,128)(2,1)S(1)} %get-tuple-element.43.high, bf16[256,4096]{1,0:T(8,128)(2,1)} %get-tuple-element.44.mid, bf16[256,4096]{1,0:T(8,128)(2,1)} %get-tuple-element.45.low), custom_call_target="tpu_custom_call" | custom-call | tf_op jit(solution)/shard_map/first_sums/pallas_call | solution.py:450
  65.9 14.0 %all_to_all.26 = f32[32,16,128]{2,1,0:T(8,128)S(1)} all-to-all(f32[32,16,128]{2,1,0:T(8,128)S(1)} %bitcast.13), channel_id=1, replica_groups=mesh['wide'=16,'narrow'=2] {'wide','narrow'}, dimensions={0} | all-to-all | bytes 524288 | tf_op jit(solution)/shard_map/all_to_all | solution.py:31
  79.9 12.8 %all_to_all.27 = f32[32,16,128]{2,1,0:T(8,128)S(1)} all-to-all(f32[32,16,128]{2,1,0:T(8,128)S(1)} %broadcast_in_dim.6), channel_id=1, replica_groups=mesh['wide'=16,'narrow'=2] {'wide','narrow'}, dimensions={0} | all-to-all | bytes 524288 | tf_op jit(solution)/shard_map/all_to_all | solution.py:33
  92.7 1.4 %coefficients_of.1 = (f32[48,256]{1,0:T(8,128)}, bf16[144,256]{1,0:T(8,128)(2,1)S(1)}, f32[48,128]{1,0:T(8,128)S(1)}, f32[1]{0:T(128)}) custom-call(f32[512,128]{1,0:T(8,128)S(1)} %bitcast.12), custom_call_target="tpu_custom_call" | custom-call | tf_op jit(solution)/shard_map/coefficients_of/pallas_call | solution.py:511
  94.8 4.8 %cleaned.3 = (f32[48,32,128]{2,1,0:T(8,128)}, f32[1,48]{1,0:T(1,128)}) custom-call(f32[1536,128]{1,0:T(8,128)S(1)} %bitcast.16, bf16[144,256]{1,0:T(8,128)(2,1)S(1)} %get-tuple-element.46.coef, f32[48,128]{1,0:T(8,128)S(1)} %get-tuple-element.52.mean_ref, bf16[256,4096]{1,0:T(8,128)(2,1)S(1)} %get-tuple-element.43.high, ...), custom_call_target="tpu_custom_call" | custom-call | tf_op jit(solution)/shard_map/cleaned/pallas_call | solution.py:565
  (3 shorter events, 0.1 us)
Async XLA Ops:
  2.4 23.4 %all-to-all-start.1 = ((f32[16,2,4,8,128]{4,3,2,1,0:T(8,128)}), f32[16,2,4,8,128]{4,3,2,1,0:T(8,128)S(1)}, u32[]{:S(2)}, u32[]{:S(2)}) async-start(f32[16,2,4,8,128]{4,3,2,1,0:T(8,128)} %packed.1), calls=%async_computation.1 | async-start | bytes 1048576 | tf_op jit(solution)/shard_map/all_to_all | solution.py:289
  10.8 2.2 %copy-start = (f32[256,4,8,128]{3,2,1,0:T(8,128)S(1)}, f32[256,4,8,128]{3,2,1,0:T(8,128)}, u32[]{:S(2)}) copy-start(f32[256,4,8,128]{3,2,1,0:T(8,128)} %param.7) | copy-start | bytes 12582916
  13.0 14.8 %copy-start.1 = (f32[3]{0:T(128)S(1)}, f32[3]{0:T(128)}, u32[]{:S(2)}) copy-start(f32[3]{0:T(128)} %shift_ref.1) | copy-start | bytes 40
  25.8 1.9 %collective-permute-start = (f32[16,2,4,8,128]{4,3,2,1,0:T(8,128)S(1)}, f32[16,2,4,8,128]{4,3,2,1,0:T(8,128)S(1)}, u32[]{:S(2)}, u32[]{:S(2)}) collective-permute-start(f32[16,2,4,8,128]{4,3,2,1,0:T(8,128)S(1)} %all-to-all-done.1.refs_0_), channel_id=1, source_target_pairs={{1,0},{0,1},{3,2},{2,3},{5,4},{4,5},{7,6},{6,7},{9,8},{8,9},{11,10... | collective-permute-start | bytes 1572872 | tf_op jit(solution)/shard_map/ppermute | solution.py:293
  37.6 23.5 %all-to-all-start.2 = ((f32[32,6,8,128]{3,2,1,0:T(8,128)}), f32[32,6,8,128]{3,2,1,0:T(8,128)S(1)}, u32[]{:S(2)}, u32[]{:S(2)}) async-start(f32[32,6,8,128]{3,2,1,0:T(8,128)} %bitcast.3), calls=%async_computation.2 | async-start | bytes 1572864 | tf_op jit(solution)/shard_map/all_to_all | solution.py:309
